TPU v7x, 32 devices: a whole 2x2x4 slice. The times are simulated.
32 devices in a mesh: shot: 8 (over z, y), depth: 4 (over x, core).
Axes of the slice: x: 2, y: 2, z: 4, core: 2. Of those that a mesh axis runs over, the one named last changes fastest.
Arguments:
- correlation: float32 [16, 16, 32, 512], P('shot', None, None, 'depth'), may hold values from -6 to 6
- illumination: float32 [16, 16, 32, 512], P('shot', None, None, 'depth'), may hold values from 0.25 to 4
- aperture: int32 [16, 4], P('shot'), may hold values from 0 to 32, as said below
Outputs:
- stack: float32 [16, 32, 512], P('shot', None, 'depth')
Inputs may be any that keep to these rules, and one draw needn't show every extreme that they name: For every shot, 0 <= aperture[s,0] < aperture[s,1] <= 16 and 0 <= aperture[s,2] < aperture[s,3] <= 32; each box spans a quarter to a half of the grid along each of the two dimensions.
All inputs are finite; a program needn't handle non-finite values.
Results may differ from a plain program's by a relative error of at most 0.0003.
Values sent between devices are 32-bit elements.
A program may use at most 64 MiB of HBM per device.

v0:
```python
import functools
import math

import jax
import jax.numpy as jnp
from jax import lax
from jax.experimental import pallas as pl
from jax.experimental.pallas import tpu as pltpu
from jax.sharding import PartitionSpec as P

MESH = pl.DeviceIdType.MESH
LANES = 128
SUBLANES = 8
NEAR = 2


def kernel(dims, corr_hbm, ill_hbm, box, out_ref, corr, ill, norm, edge_out, edge_in, send, recv,
           note_out, note_in, load_sem, edge_send, edge_recv, bulk_send, bulk_recv, note_send, note_recv):
    shots, rows, cols, slab, groups, slabs, owned, width, total_shots, cells = dims
    tiles = cols // SUBLANES
    per_row = shots * tiles
    rows_per_pack = LANES // per_row
    packs = rows // rows_per_pack
    per_owner = owned * per_row
    owners_per_pack = LANES // per_owner
    group = lax.axis_index("shot")
    depth = lax.axis_index("depth")

    barrier = pltpu.get_barrier_semaphore()
    for j in range(1, groups):
        pl.semaphore_signal(barrier, inc=1, device_id={"shot": lax.rem(group + j, groups)}, device_id_type=MESH)
    for j in range(1, slabs):
        pl.semaphore_signal(barrier, inc=1, device_id={"depth": lax.rem(depth + j, slabs)}, device_id_type=MESH)

    loads = []
    for s in range(shots):
        pair = (
            pltpu.make_async_copy(corr_hbm.at[s], corr.at[s], load_sem.at[0, s]),
            pltpu.make_async_copy(ill_hbm.at[s], ill.at[s], load_sem.at[1, s]),
        )
        for copy in pair:
            copy.start()
        loads.append(pair)

    lane = lax.broadcasted_iota(jnp.int32, (SUBLANES, LANES), 1)
    lane_row = lax.broadcasted_iota(jnp.int32, (cols, slab), 1)
    col = lax.broadcasted_iota(jnp.int32, (cols, slab), 0)
    plane = jnp.zeros((cols, slab), jnp.float32)
    edge = jnp.zeros((SUBLANES, slab), jnp.float32)
    for s in range(shots):
        norm[s, 0, pl.ds(SUBLANES, cols)] = plane
        norm[s, rows + 1, pl.ds(SUBLANES, cols)] = plane

    col_mask = [(col >= box[s, 2]) & (col < box[s, 3]) for s in range(shots)]
    for pair in loads:
        for copy in pair:
            copy.wait()

    def pack(value, i, s, low, high):
        for c in range(tiles):
            k = (i * shots + s) * tiles + c
            piece = value[c * SUBLANES:(c + 1) * SUBLANES]
            low = jnp.where(lane == k, pltpu.roll(piece, k, 1), low)
            high = jnp.where(lane == k, pltpu.roll(piece, (k + 1) % LANES, 1), high)
        return low, high

    def normalise(p, carry):
        low = edge
        high = edge
        for i in range(rows_per_pack):
            r = p * rows_per_pack + i
            for s in range(shots):
                inside = col_mask[s] & (r >= box[s, 0]) & (r < box[s, 1])
                value = jnp.where(inside, corr[s, r], 0.0) / (ill[s, r] + 0.1)
                norm[s, r + 1, pl.ds(0, SUBLANES)] = edge
                norm[s, r + 1, pl.ds(SUBLANES, cols)] = value
                norm[s, r + 1, pl.ds(SUBLANES + cols, SUBLANES)] = edge
                low, high = pack(value, i, s, low, high)
        edge_out[p] = low
        edge_out[packs + p] = high
        return carry

    lax.fori_loop(0, packs, normalise, 0)

    fold_mask = col < cols - width
    not_first = lane_row > 0
    not_last = lane_row < slab - 1

    def filtered(p, energies):
        energies = list(energies)
        low = edge
        high = edge
        for i in range(rows_per_pack):
            r = p * rows_per_pack + i
            owner = p * (rows_per_pack // owned) + i // owned
            for s in range(shots):
                value = norm[s, r + 1, pl.ds(SUBLANES, cols)]
                beside = norm[s, r + 2, pl.ds(SUBLANES, cols)] + norm[s, r, pl.ds(SUBLANES, cols)]
                beside = beside + norm[s, r + 1, pl.ds(SUBLANES + 1, cols)]
                beside = beside + norm[s, r + 1, pl.ds(SUBLANES - 1, cols)]
                before = jnp.where(not_first, pltpu.roll(value, 1, 1), 0.0)
                after = jnp.where(not_last, pltpu.roll(value, slab - 1, 1), 0.0)
                result = 6.0 * value - (beside + before + after)
                energies[s] = energies[s] + result * result
                low, high = pack(result, i, s, low, high)
                other = pltpu.roll(result, cols - width, 0)
                folded = result + jnp.where(fold_mask, other, 0.0)
                send[owner, pl.ds((s * owned + i % owned) * width, width)] = folded[:width]
        edge_out[2 * packs + p] = low
        edge_out[3 * packs + p] = high
        return tuple(energies)

    energies = lax.fori_loop(0, packs, filtered, (plane,) * shots)

    def total(value):
        return jnp.sum(jnp.sum(value, axis=0, keepdims=True), axis=1, keepdims=True)

    shot_row = lax.broadcasted_iota(jnp.int32, (SUBLANES, LANES), 0)
    message = edge
    for s in range(shots):
        message = jnp.where(shot_row == s, total(energies[s]), message)
    edge_out[4 * packs] = message

    pl.semaphore_wait(barrier, slabs + groups - 2)

    edges = []
    for j in range(1, slabs):
        copy = pltpu.make_async_remote_copy(
            src_ref=edge_out, dst_ref=edge_in.at[j - 1],
            send_sem=edge_send.at[j - 1], recv_sem=edge_recv.at[j - 1],
            device_id={"depth": lax.rem(depth + j, slabs)}, device_id_type=MESH)
        copy.start()
        edges.append(copy)

    order = sorted(range(1, groups), key=lambda j: abs(2 * j - groups))
    pair = 2 if groups % 2 == 0 else 1

    def distance(j):
        target = lax.rem(group + j, groups)
        return jnp.abs(target // pair - group // pair) + jnp.abs(lax.rem(target, pair) - lax.rem(group, pair))

    def start_bulk(far):
        for level in range(3, -1, -1):
            if (level >= NEAR) == far:
                for j in order:
                    near = distance(j)
                    pl.when((near > level) & ((near <= level + 1) | (level == 3)))(bulk[j].start)

    bulk = {}
    for j in order:
        target = lax.rem(group + j, groups)
        bulk[j] = pltpu.make_async_remote_copy(
            src_ref=send.at[target], dst_ref=recv.at[j - 1],
            send_sem=bulk_send.at[j - 1], recv_sem=bulk_recv.at[j - 1],
            device_id={"shot": target}, device_id_type=MESH)
    start_bulk(True)

    for copy in edges:
        copy.wait()
    places = [edge_out] + [edge_in.at[slabs - i - 1] for i in range(1, slabs)]
    for i in range(1, slabs):
        message = message + places[i][4 * packs]
    cross = edge
    for i in range(slabs):
        here, there = places[i], places[(i + 1) % slabs]
        part = edge
        for p in range(packs):
            above = there[p]
            below = here[packs + p]
            part = part + above * (above - 2.0 * here[3 * packs + p])
            part = part + below * (below - 2.0 * there[2 * packs + p])
        cross = cross + jnp.where(lax.rem(depth + i, slabs) < slabs - 1, part, 0.0)
    lane_shot = lax.rem(lane // tiles, shots)
    for s in range(shots):
        message = message + jnp.where(shot_row == s, total(jnp.where(lane_shot == s, cross, 0.0)), 0.0)
    message = message / cells
    for s in range(shots):
        message = jnp.where(shot_row == shots + s, (box[s, 2] - 1).astype(jnp.float32), message)
    for p in range(packs):
        low = jnp.where(depth > 0, places[slabs - 1][packs + p], 0.0)
        high = jnp.where(depth < slabs - 1, places[1][p], 0.0)
        for q in range(owners_per_pack):
            offset = q * per_owner
            halo = jnp.where(lane < per_owner, pltpu.roll(low, (LANES - offset) % LANES, 1),
                             pltpu.roll(high, (LANES + per_owner - offset) % LANES, 1))
            owner = p * owners_per_pack + q
            note_out[owner, 0] = jnp.where(lane < 2 * per_owner, halo, 0.0)
            note_out[owner, 1] = message
    notes = {}
    for j in order:
        target = lax.rem(group + j, groups)
        notes[j] = pltpu.make_async_remote_copy(
            src_ref=note_out.at[target], dst_ref=note_in.at[j - 1],
            send_sem=note_send.at[j - 1], recv_sem=note_recv.at[j - 1],
            device_id={"shot": target}, device_id_type=MESH)
    for level in range(3, -1, -1):
        for j in order:
            near = distance(j)
            pl.when((near > level) & ((near <= level + 1) | (level == 3)))(notes[j].start)
    start_bulk(False)
    for j in order:
        notes[j].wait()
    peak = jnp.where(shot_row < shots, message, 0.0)
    for j in range(1, groups):
        peak = jnp.maximum(peak, jnp.where(shot_row < shots, note_in[j - 1, 1], 0.0))
    peak = jnp.max(peak, axis=0, keepdims=True)

    scale = 1.0 / math.sqrt(total_shots)
    col_float = col.astype(jnp.float32)

    def unfold(block, note, sums):
        row = note[1]
        weight = scale / jnp.sqrt(jnp.where(shot_row < shots, row, 0.0) + 0.5 * peak + 1.0)
        by_lane = edge
        for s in range(shots):
            first = row[shots + s:shots + s + 1]
            inside = (col_float >= first) & (col_float < first + width)
            factor = jnp.where(inside, weight[s:s + 1], 0.0)
            by_lane = jnp.where(lane_shot == s, weight[s:s + 1], by_lane)
            for i in range(owned):
                value = block[pl.ds((s * owned + i) * width, width)]
                sums[i] = sums[i] + factor * jnp.concatenate([value, value[:cols - width]], axis=0)
        sums[owned] = sums[owned] + by_lane * note[0]
        return sums

    sums = unfold(send.at[group], note_out.at[group], [plane] * owned + [edge])
    for j in order:
        bulk[j].wait()
        sums = unfold(recv.at[j - 1], note_in.at[j - 1], sums)
    halo = sums[owned]
    for s in range(1, shots):
        halo = halo + pltpu.roll(sums[owned], LANES - s * tiles, 1)
    for i in range(owned):
        lows = []
        highs = []
        for c in range(tiles):
            k = i * per_row + c
            lows.append(pltpu.roll(halo, (LANES - k) % LANES, 1))
            highs.append(pltpu.roll(halo, LANES - 1 - per_owner - k, 1))
        value = sums[i] - jnp.where(not_first, 0.0, jnp.concatenate(lows, axis=0))
        out_ref[i] = value - jnp.where(not_last, 0.0, jnp.concatenate(highs, axis=0))


def on_device(correlation, illumination, aperture):
    shots, rows, cols, slab = correlation.shape
    groups = lax.axis_size("shot")
    slabs = lax.axis_size("depth")
    owned = rows // groups
    width = min(cols, cols // 2 + 2)
    dims = (shots, rows, cols, slab, groups, slabs, owned, width, shots * groups, rows * cols * slab * slabs)
    packs = rows * shots * (cols // SUBLANES) // LANES
    edges = (4 * packs + 1, SUBLANES, LANES)
    block = (shots * owned * width, slab)
    f32 = jnp.float32
    dma = pltpu.SemaphoreType.DMA
    return pl.pallas_call(
        functools.partial(kernel, dims),
        out_shape=pltpu.VMEM((owned, cols, slab), f32),
        in_specs=[
            pl.BlockSpec(memory_space=pl.ANY),
            pl.BlockSpec(memory_space=pl.ANY),
            pl.BlockSpec(memory_space=pltpu.SMEM),
        ],
        out_specs=pl.BlockSpec(memory_space=pltpu.VMEM),
        scratch_shapes=[
            pltpu.VMEM((shots, rows, cols, slab), f32),
            pltpu.VMEM((shots, rows, cols, slab), f32),
            pltpu.VMEM((shots, rows + 2, cols + 2 * SUBLANES, slab), f32),
            pltpu.VMEM(edges, f32),
            pltpu.VMEM((slabs - 1,) + edges, f32),
            pltpu.VMEM((groups,) + block, f32),
            pltpu.VMEM((groups - 1,) + block, f32),
            pltpu.VMEM((groups, 2, SUBLANES, LANES), f32),
            pltpu.VMEM((groups - 1, 2, SUBLANES, LANES), f32),
            dma((2, shots)),
            dma((slabs - 1,)),
            dma((slabs - 1,)),
            dma((groups - 1,)),
            dma((groups - 1,)),
            dma((groups - 1,)),
            dma((groups - 1,)),
        ],
        compiler_params=pltpu.CompilerParams(collective_id=0, has_side_effects=True),
    )(correlation, illumination, aperture)


def solution(mesh):
    return jax.shard_map(
        on_device,
        mesh=mesh,
        in_specs=(P("shot", None, None, "depth"), P("shot", None, None, "depth"), P("shot", None)),
        out_specs=P("shot", None, "depth"),
        check_vma=False,
    )
```

profile of v0, /device:TPU:0, one launch (start us, length us, event | category | flops | bytes accessed | tf_op | source)
XLA Modules:
  0.0 18.0 jit_solution(2797620974328496222)
XLA Ops:
  0.0 17.3 %shard_map.37 = f32[2,32,128]{2,1,0:T(8,128)S(1)} custom-call(f32[2,16,32,128]{3,2,1,0:T(8,128)} %corr_hbm.1, f32[2,16,32,128]{3,2,1,0:T(8,128)} %ill_hbm.1, s32[2,4]{1,0:T(2,128)} %box.1), custom_call_target="tpu_custom_call" | custom-call | tf_op jit(solution)/shard_map/pallas_call | solution.py:256
  17.3 0.6 %copy.5 = f32[2,32,128]{2,1,0:T(8,128)} copy(f32[2,32,128]{2,1,0:T(8,128)S(1)} %shard_map.37) | data formatting | bytes 65536
where the time goes:
time: 18.1 us; the launch traced here: 18 us
  Pallas kernels  17.3 us (96%)
  local copies, waits for them, and re-layouts  0.62 us (3%)
    pallas_call x1, Pallas kernels, on_device(): pl.pallas_call(functools.partial(kernel, dims), out_shape=pltpu.VMEM((own...  17.3 us
    unnamed x1, local copies, waits for them, and re-layouts  0.62 us

commit v1 on v0

v1 whole, which is shorter than its diff:
```python
import functools
import math

import jax
import jax.numpy as jnp
from jax import lax
from jax.experimental import pallas as pl
from jax.experimental.pallas import tpu as pltpu
from jax.sharding import PartitionSpec as P

MESH = pl.DeviceIdType.MESH
LANES = 128
SUBLANES = 8


def kernel(dims, corr_hbm, ill_hbm, box_hbm, out_ref, box, corr, ill, norm, edge_out, edge_in, send, recv, side_out, side_in,
           place_out, place, message, inbox, spread, load_sem, box_sem, ready, edge_send, edge_recv, bulk_send, bulk_recv,
           side_send, side_recv, place_send, place_recv, note_send, note_recv):
    shots, rows, cols, slab, groups, slabs, owned, cells = dims
    half = cols // 2
    tiles = half // SUBLANES
    devices = groups * slabs
    per_pack = LANES // 2
    group = lax.axis_index("shot")
    depth = lax.axis_index("depth")
    place_in_order = group * slabs + depth

    box_copy = pltpu.make_async_copy(box_hbm, box, box_sem)
    box_copy.start()
    loads = []
    for s in range(shots):
        for index, (source, target) in enumerate(((corr_hbm, corr), (ill_hbm, ill))):
            copy = pltpu.make_async_copy(source.at[s], target.at[s], load_sem.at[index, s])
            copy.start()
            loads.append(copy)

    def at(t):
        return {"shot": lax.div(t, slabs), "depth": lax.rem(t, slabs)}

    barrier = pltpu.get_barrier_semaphore()

    def greet(t, carry):
        pl.semaphore_signal(barrier, inc=1, device_id=at(t), device_id_type=MESH)
        return carry

    lax.fori_loop(place_in_order + 1, devices, greet, 0)

    lane = lax.broadcasted_iota(jnp.int32, (SUBLANES, LANES), 1)
    sub = lax.broadcasted_iota(jnp.int32, (SUBLANES, LANES), 0)
    zero = jnp.zeros((SUBLANES, slab), jnp.float32)
    for s in range(shots):
        for r in (0, rows + 1):
            for t in range(tiles + 2):
                norm[s, r, pl.ds(t * SUBLANES, SUBLANES)] = zero
    packs = edge_out.shape[0]

    @pl.when(depth == 0)
    def _():
        for p in range(packs):
            edge_in[0, p] = zero

    @pl.when(depth == slabs - 1)
    def _():
        for p in range(packs):
            edge_in[1, p] = zero

    @pl.when(place_in_order > 0)
    def _():
        pl.semaphore_wait(barrier, place_in_order)

    def answer(i, carry):
        t = place_in_order - 1 - i
        pl.semaphore_signal(ready.at[group], inc=1, device_id=at(t), device_id_type=MESH)
        return carry

    lax.fori_loop(0, place_in_order, answer, 0)

    box_copy.wait()
    lower = []
    upper = []
    start = []
    for s in range(shots):
        first, last = box[s, 2], box[s, 3]
        start.append(jnp.minimum(first, half))
        lower.append([(sub + t * SUBLANES >= first) & (sub + t * SUBLANES < last) for t in range(tiles)])
        upper.append([(sub + t * SUBLANES + half >= first) & (sub + t * SUBLANES + half < last) for t in range(tiles)])
        place_out[pl.ds(s, 1)] = jnp.full((1, LANES), start[s].astype(jnp.float32))
    for copy in loads:
        copy.wait()

    row_index = lax.broadcasted_iota(jnp.int32, (rows, slab), 0)
    energies = []
    for s in range(shots):
        in_rows = (row_index >= box[s, 0]) & (row_index < box[s, 1])
        energy = None
        for side, column in enumerate((start[s], start[s] + half - 1)):
            in_box = (column >= box[s, 2]) & (column < box[s, 3])
            value = jnp.where(in_rows & in_box, corr[s, :, column], 0.0) / (ill[s, :, column] + 0.1)
            side_out[2 * s + side] = 0.0 - value
            in_grid = (start[s] > 0) if side == 0 else (start[s] < cols - half)
            kept = jnp.where(in_grid, value, 0.0)
            kept = kept * kept
            energy = kept if energy is None else energy + kept
        while energy.shape[0] > SUBLANES:
            energy = energy[:energy.shape[0] // 2] + energy[energy.shape[0] // 2:]
        energies.append(energy)

    def lane_of(r, s, t):
        k = (r * shots + s) * tiles + t
        return k // per_pack, 2 * (k % per_pack)

    packed = [zero] * packs
    for r in range(rows):
        for s in range(shots):
            in_row = (r >= box[s, 0]) & (r < box[s, 1])
            parts = []
            for t in range(tiles):
                here = pl.ds(t * SUBLANES, SUBLANES)
                there = pl.ds(t * SUBLANES + half, SUBLANES)
                top = jnp.where(upper[s][t], corr[s, r, there], corr[s, r, here])
                top = jnp.where((lower[s][t] | upper[s][t]) & in_row, top, 0.0)
                value = top / (jnp.where(upper[s][t], ill[s, r, there], ill[s, r, here]) + 0.1)
                parts.append(value)
                p, k = lane_of(r, s, t)
                packed[p] = jnp.where(lane // 2 == k // 2, pltpu.roll(value, k + 1, 1), packed[p])
            for t, value in enumerate([parts[-1]] + parts + [parts[0]]):
                norm[s, r + 1, pl.ds(t * SUBLANES, SUBLANES)] = value
    for p in range(packs):
        edge_out[p] = packed[p]

    def edge_copy(side):
        return pltpu.make_async_remote_copy(
            src_ref=edge_out, dst_ref=edge_in.at[1 - side], send_sem=edge_send.at[side],
            recv_sem=edge_recv.at[1 - side], device_id={"depth": depth + (1 if side else -1)}, device_id_type=MESH)

    @pl.when(depth > 0)
    def _():
        edge_copy(0).start()

    @pl.when(depth < slabs - 1)
    def _():
        pl.semaphore_wait(ready.at[group], slabs - 1 - depth)
        edge_copy(1).start()

    @pl.when(depth > 0)
    def _():
        edge_copy(0).wait_send()
        edge_copy(1).wait_recv()

    @pl.when(depth < slabs - 1)
    def _():
        edge_copy(1).wait_send()
        edge_copy(0).wait_recv()

    no_before = [[sub + t * SUBLANES == lax.rem(start[s], half) for t in range(tiles)] for s in range(shots)]
    no_after = [[sub + t * SUBLANES == lax.rem(start[s] + half - 1, half) for t in range(tiles)] for s in range(shots)]
    halo = [jnp.where(lane % 2 == 0, edge_in[0, p], edge_in[1, p]) for p in range(packs)]
    for r in range(rows):
        owner, i = r // owned, r % owned
        for s in range(shots):
            for t in range(tiles):
                base = SUBLANES + t * SUBLANES
                value = norm[s, r + 1, pl.ds(base, SUBLANES)]
                beside = norm[s, r, pl.ds(base, SUBLANES)] + norm[s, r + 2, pl.ds(base, SUBLANES)]
                beside = beside + jnp.where(no_before[s][t], 0.0, norm[s, r + 1, pl.ds(base - 1, SUBLANES)])
                beside = beside + jnp.where(no_after[s][t], 0.0, norm[s, r + 1, pl.ds(base + 1, SUBLANES)])
                p, k = lane_of(r, s, t)
                near = pltpu.roll(halo[p], LANES - 1 - k, 1)
                left = jnp.where(lane == LANES - 1, near, value)
                right = jnp.where(lane == 0, near, value)
                beside = beside + pltpu.roll(left, 1, 1) + pltpu.roll(right, LANES - 1, 1)
                result = 6.0 * value - beside
                energies[s] = energies[s] + result * result
                send[owner, pl.ds((s * owned + i) * half + t * SUBLANES, SUBLANES)] = result

    def total(value):
        return jnp.sum(jnp.sum(value, axis=0, keepdims=True), axis=1, keepdims=True)

    note = jnp.zeros((1, LANES), jnp.float32)
    gap = LANES // shots
    lane_row = lax.broadcasted_iota(jnp.int32, (1, LANES), 1)
    for s in range(shots):
        note = jnp.where(lane_row // gap == s, total(energies[s]), note)
    message[pl.ds(0, 1)] = note / cells

    slot = depth * groups + group
    own_note = pltpu.make_async_copy(message.at[pl.ds(0, 1)], inbox.at[pl.ds(slot, 1)], note_recv)
    own_note.start()

    def tell(g, d):
        pltpu.make_async_remote_copy(
            src_ref=message.at[pl.ds(0, 1)], dst_ref=inbox.at[pl.ds(slot, 1)], send_sem=note_send, recv_sem=note_recv,
            device_id={"shot": g, "depth": d}, device_id_type=MESH).start()

    def bulk(g, origin):
        return pltpu.make_async_remote_copy(
            src_ref=send.at[g], dst_ref=recv.at[origin], send_sem=bulk_send.at[g], recv_sem=bulk_recv.at[origin],
            device_id={"shot": g}, device_id_type=MESH)

    def side_copy(g, origin):
        return pltpu.make_async_remote_copy(
            src_ref=side_out.at[:, pl.ds(g * owned, owned)], dst_ref=side_in.at[origin], send_sem=side_send.at[g],
            recv_sem=side_recv.at[origin], device_id={"shot": g}, device_id_type=MESH)

    def place_copy(g, origin):
        return pltpu.make_async_remote_copy(
            src_ref=place_out, dst_ref=place.at[origin], send_sem=place_send.at[g], recv_sem=place_recv.at[origin],
            device_id={"shot": g}, device_id_type=MESH)

    for g in range(groups):
        @pl.when(g < group)
        def _():
            for d in range(slabs):
                tell(g, d)
    for d in range(slabs):
        @pl.when(d != depth)
        def _():
            tell(group, d)
    for g in range(groups):
        @pl.when(g < group)
        def _():
            place_copy(g, group).start()
            side_copy(g, group).start()
            bulk(g, group).start()
    for g in range(1, groups):
        @pl.when(g > group)
        def _():
            pl.semaphore_wait(ready.at[g], slabs)
            for d in range(slabs):
                tell(g, d)
            place_copy(g, group).start()
            side_copy(g, group).start()
            bulk(g, group).start()

    recv[group] = send[group]
    side_in[group] = side_out[:, pl.ds(group * owned, owned)]
    place[group] = place_out[...]

    col = [(sub + t * SUBLANES).astype(jnp.float32) for t in range(2 * tiles)]
    for g in range(groups):
        @pl.when(g != group)
        def _():
            place_copy(g, g).wait_recv()
            side_copy(g, g).wait_recv()
            bulk(g, g).wait_recv()

        for s in range(shots):
            first = place[g, pl.ds(s, 1)]
            masks = []
            for t in range(2 * tiles):
                offset = col[t] - first
                masks.append((offset == -1.0, offset == float(half), (offset >= -1.0) & (offset <= float(half))))
            for i in range(owned):
                index = s * owned + i
                low = side_in[g, 2 * s, pl.ds(i, 1)]
                high = side_in[g, 2 * s + 1, pl.ds(i, 1)]
                for t in range(2 * tiles):
                    at_low, at_high, inside = masks[t]
                    value = recv[g, pl.ds(index * half + (t % tiles) * SUBLANES, SUBLANES)]
                    value = jnp.where(at_low, low, jnp.where(at_high, high, value))
                    spread[g, s, i, pl.ds(t * SUBLANES, SUBLANES)] = jnp.where(inside, value, 0.0)

    pltpu.make_async_copy(inbox, inbox, note_recv).wait()
    meansq = inbox[pl.ds(0, groups)]
    for d in range(1, slabs):
        meansq = meansq + inbox[pl.ds(d * groups, groups)]
    peak = jnp.max(meansq, axis=0, keepdims=True)
    turned = peak
    for s in range(1, shots):
        turned = jnp.maximum(turned, pltpu.roll(peak, s * gap, 1))
    weight = (1.0 / math.sqrt(shots * groups)) / jnp.sqrt(meansq + 0.5 * turned + 1.0)
    lane_group = lax.broadcasted_iota(jnp.int32, (groups, LANES), 1) // gap
    sums = [[zero] * (2 * tiles) for i in range(owned)]
    for s in range(shots):
        factor = weight
        for j in range(1, shots):
            factor = jnp.where(lane_group == (s + j) % shots, pltpu.roll(weight, j * gap, 1), factor)
        for g in range(groups):
            for i in range(owned):
                for t in range(2 * tiles):
                    sums[i][t] = sums[i][t] + factor[g:g + 1] * spread[g, s, i, pl.ds(t * SUBLANES, SUBLANES)]
    for i in range(owned):
        for t in range(2 * tiles):
            out_ref[i, pl.ds(t * SUBLANES, SUBLANES)] = sums[i][t]

    pltpu.make_async_copy(inbox.at[pl.ds(0, devices - 1)], inbox.at[pl.ds(0, devices - 1)], note_send).wait()
    for g in range(groups):
        @pl.when(g != group)
        def _():
            place_copy(g, g).wait_send()
            side_copy(g, g).wait_send()
            bulk(g, g).wait_send()


def on_device(correlation, illumination, aperture):
    shots, rows, cols, slab = correlation.shape
    groups = lax.axis_size("shot")
    slabs = lax.axis_size("depth")
    owned = rows // groups
    half = cols // 2
    tiles = half // SUBLANES
    dims = (shots, rows, cols, slab, groups, slabs, owned, rows * cols * slab * slabs)
    packs = -(-rows * shots * tiles // (LANES // 2))
    block = (shots * owned * half, slab)
    f32 = jnp.float32
    dma = pltpu.SemaphoreType.DMA
    return pl.pallas_call(
        functools.partial(kernel, dims),
        out_shape=pltpu.VMEM((owned, cols, slab), f32),
        in_specs=[pl.BlockSpec(memory_space=pl.ANY)] * 3,
        out_specs=pl.BlockSpec(memory_space=pltpu.VMEM),
        scratch_shapes=[
            pltpu.SMEM(aperture.shape, jnp.int32),
            pltpu.VMEM((shots, rows, cols, slab), f32),
            pltpu.VMEM((shots, rows, cols, slab), f32),
            pltpu.VMEM((shots, rows + 2, half + 2 * SUBLANES, slab), f32),
            pltpu.VMEM((packs, SUBLANES, LANES), f32),
            pltpu.VMEM((2, packs, SUBLANES, LANES), f32),
            pltpu.VMEM((groups,) + block, f32),
            pltpu.VMEM((groups,) + block, f32),
            pltpu.VMEM((2 * shots, rows, slab), f32),
            pltpu.VMEM((groups, 2 * shots, owned, slab), f32),
            pltpu.VMEM((shots, LANES), f32),
            pltpu.VMEM((groups, shots, LANES), f32),
            pltpu.VMEM((SUBLANES, LANES), f32),
            pltpu.VMEM((slabs * groups, LANES), f32),
            pltpu.VMEM((groups, shots, owned, cols, slab), f32),
            dma((2, shots)),
            dma,
            pltpu.SemaphoreType.REGULAR((groups,)),
            dma((2,)),
            dma((2,)),
            dma((groups,)),
            dma((groups,)),
            dma((groups,)),
            dma((groups,)),
            dma((groups,)),
            dma((groups,)),
            dma,
            dma,
        ],
        compiler_params=pltpu.CompilerParams(collective_id=0, has_side_effects=True),
    )(correlation, illumination, aperture)


def solution(mesh):
    return jax.shard_map(
        on_device,
        mesh=mesh,
        in_specs=(P("shot", None, None, "depth"), P("shot", None, None, "depth"), P("shot", None)),
        out_specs=P("shot", None, "depth"),
        check_vma=False,
    )
```

time: 18.1 us -> 15.9 us (0.88)
  the two profiles are of different devices: /device:TPU:0 before, /device:TPU:13 now
where the time goes in v1:
time: 15.9 us; the launch traced here: 15.7 us
  Pallas kernels  15.1 us (95%)
  local copies, waits for them, and re-layouts  0.62 us (4%)
    pallas_call x1, Pallas kernels, on_device(): pl.pallas_call(functools.partial(kernel, dims), out_shape=pltpu.VMEM((own...  15.1 us
    unnamed x1, local copies, waits for them, and re-layouts  0.62 us

profile of v1, /device:TPU:13, one launch (start us, length us, event | category | flops | bytes accessed | tf_op | source)
XLA Modules:
  0.0 15.7 jit_solution(12584772988648626133)
XLA Ops:
  0.0 15.1 %shard_map.37 = f32[2,32,128]{2,1,0:T(8,128)S(1)} custom-call(f32[2,16,32,128]{3,2,1,0:T(8,128)} %corr_hbm.1, f32[2,16,32,128]{3,2,1,0:T(8,128)} %ill_hbm.1, s32[2,4]{1,0:T(2,128)} %box_hbm.1), custom_call_target="tpu_custom_call" | custom-call | tf_op jit(solution)/shard_map/pallas_call | solution.py:307
  15.1 0.6 %copy.5 = f32[2,32,128]{2,1,0:T(8,128)} copy(f32[2,32,128]{2,1,0:T(8,128)S(1)} %shard_map.37) | data formatting | bytes 65536

commit v2 on v1

v2 whole, which is shorter than its diff:
```python
import functools
import math

import jax
import jax.numpy as jnp
from jax import lax
from jax.experimental import pallas as pl
from jax.experimental.pallas import tpu as pltpu
from jax.sharding import PartitionSpec as P

MESH = pl.DeviceIdType.MESH
LANES = 128
SUBLANES = 8
EARLY = 1


def kernel(dims, corr_hbm, ill_hbm, box_hbm, out_ref, box, raw, norm, centre, edge_out, edge_in, halo_out, halo_in, halves, send, recv, message, inbox, spread,
           load_sem, box_sem, ready, passed, edge_send, edge_recv, bulk_send, bulk_recv, halo_send, halo_recv, note_send, note_recv):
    shots, rows, cols, slab, groups, slabs, owned, cells = dims
    half = cols // 2
    tiles = half // SUBLANES
    devices = groups * slabs
    per_pack = LANES // 2
    per_owner = owned * shots * tiles
    group = lax.axis_index("shot")
    depth = lax.axis_index("depth")
    border = shots * owned * half
    placed = border + 2 * shots * owned
    corr, ill = raw.at[0], raw.at[1]

    box_copy = pltpu.make_async_copy(box_hbm, box, box_sem)
    box_copy.start()
    for s in range(shots):
        for source, target in ((corr_hbm, corr), (ill_hbm, ill)):
            pltpu.make_async_copy(source.at[s], target.at[s], load_sem).start()

    def signal(semaphore, **device):
        pl.semaphore_signal(semaphore, inc=1, device_id=device, device_id_type=MESH)

    def each(low, high, action):
        lax.fori_loop(low, high, lambda t, carry: (action(t), carry)[1], 0)

    barrier = pltpu.get_barrier_semaphore()
    each(1, slabs, lambda d: signal(barrier, depth=lax.rem(depth + d, slabs)))
    each(group + 1, groups, lambda g: signal(barrier, shot=g))

    lane = lax.broadcasted_iota(jnp.int32, (SUBLANES, LANES), 1)
    sub = lax.broadcasted_iota(jnp.int32, (SUBLANES, LANES), 0)
    zero = jnp.zeros((SUBLANES, slab), jnp.float32)
    for s in range(shots):
        for r in (0, rows + 1):
            for t in range(tiles + 2):
                norm[s, r, pl.ds(t * SUBLANES, SUBLANES)] = zero
    packs = edge_out.shape[0]

    @pl.when(depth == 0)
    def _():
        for p in range(packs):
            edge_in[0, p] = zero

    @pl.when(depth == slabs - 1)
    def _():
        for p in range(packs):
            edge_in[1, p] = zero

    box_copy.wait()
    lower = []
    upper = []
    start = []
    for s in range(shots):
        first, last = box[s, 2], box[s, 3]
        start.append(jnp.minimum(first, half))
        lower.append([(sub + t * SUBLANES >= first) & (sub + t * SUBLANES < last) for t in range(tiles)])
        upper.append([(sub + t * SUBLANES + half >= first) & (sub + t * SUBLANES + half < last) for t in range(tiles)])
    pltpu.make_async_copy(raw, raw, load_sem).wait()

    row_index = lax.broadcasted_iota(jnp.int32, (rows, slab), 0)
    energies = []
    for s in range(shots):
        in_rows = (row_index >= box[s, 0]) & (row_index < box[s, 1])
        energy = None
        for side, column in enumerate((start[s], start[s] + half - 1)):
            in_box = (column >= box[s, 2]) & (column < box[s, 3])
            value = jnp.where(in_rows & in_box, corr[s, :, column], 0.0) / (ill[s, :, column] + 0.1)
            for owner in range(groups):
                send[owner, pl.ds(border + (2 * s + side) * owned, owned)] = 0.0 - value[owner * owned:(owner + 1) * owned]
            in_grid = (start[s] > 0) if side == 0 else (start[s] < cols - half)
            kept = jnp.where(in_grid, value, 0.0)
            kept = kept * kept
            energy = kept if energy is None else energy + kept
        while energy.shape[0] > SUBLANES:
            energy = energy[:energy.shape[0] // 2] + energy[energy.shape[0] // 2:]
        energies.append(energy)
        for owner in range(groups):
            send[owner, pl.ds(placed + s, 1)] = jnp.full((1, LANES), start[s].astype(jnp.float32))

    def lane_of(r, s, t):
        k = (r * shots + s) * tiles + t
        return k // per_pack, 2 * (k % per_pack)

    packed = [zero] * packs
    for r in range(rows):
        for s in range(shots):
            in_row = (r >= box[s, 0]) & (r < box[s, 1])
            parts = []
            for t in range(tiles):
                here = pl.ds(t * SUBLANES, SUBLANES)
                there = pl.ds(t * SUBLANES + half, SUBLANES)
                top = jnp.where(upper[s][t], corr[s, r, there], corr[s, r, here])
                top = jnp.where((lower[s][t] | upper[s][t]) & in_row, top, 0.0)
                value = top / (jnp.where(upper[s][t], ill[s, r, there], ill[s, r, here]) + 0.1)
                parts.append(value)
                p, k = lane_of(r, s, t)
                packed[p] = jnp.where(lane // 2 == k // 2, pltpu.roll(value, k + 1, 1), packed[p])
                beside = jnp.where(lane > 0, pltpu.roll(value, 1, 1), 0.0)
                beside = beside + jnp.where(lane < LANES - 1, pltpu.roll(value, LANES - 1, 1), 0.0)
                centre[s, r, pl.ds(t * SUBLANES, SUBLANES)] = 6.0 * value - beside
            for t, value in enumerate([parts[-1]] + parts + [parts[0]]):
                norm[s, r + 1, pl.ds(t * SUBLANES, SUBLANES)] = value
    for p in range(packs):
        edge_out[p] = packed[p]

    def edge_copy(side):
        return pltpu.make_async_remote_copy(
            src_ref=edge_out, dst_ref=edge_in.at[1 - side], send_sem=edge_send.at[side],
            recv_sem=edge_recv.at[1 - side], device_id={"depth": depth + (1 if side else -1)}, device_id_type=MESH)

    pl.semaphore_wait(barrier, group + slabs - 1)

    @pl.when(depth > 0)
    def _():
        edge_copy(0).start()

    @pl.when(depth < slabs - 1)
    def _():
        edge_copy(1).start()

    each(0, group, lambda g: signal(ready.at[group], shot=g))
    each(1, slabs, lambda d: signal(passed, depth=lax.rem(depth + d, slabs)))

    no_before = [[sub + t * SUBLANES == lax.rem(start[s], half) for t in range(tiles)] for s in range(shots)]
    no_after = [[sub + t * SUBLANES == lax.rem(start[s] + half - 1, half) for t in range(tiles)] for s in range(shots)]
    packed = [zero] * packs
    for r in range(rows):
        owner, i = r // owned, r % owned
        for s in range(shots):
            for t in range(tiles):
                base = SUBLANES + t * SUBLANES
                beside = norm[s, r, pl.ds(base, SUBLANES)] + norm[s, r + 2, pl.ds(base, SUBLANES)]
                beside = beside + jnp.where(no_before[s][t], 0.0, norm[s, r + 1, pl.ds(base - 1, SUBLANES)])
                beside = beside + jnp.where(no_after[s][t], 0.0, norm[s, r + 1, pl.ds(base + 1, SUBLANES)])
                p, k = lane_of(r, s, t)
                result = centre[s, r, pl.ds(t * SUBLANES, SUBLANES)] - beside
                energies[s] = energies[s] + result * result
                packed[p] = jnp.where(lane // 2 == k // 2, pltpu.roll(result, k + 1, 1), packed[p])
                send[owner, pl.ds((s * owned + i) * half + t * SUBLANES, SUBLANES)] = result

    def bulk(g, origin):
        return pltpu.make_async_remote_copy(
            src_ref=send.at[g], dst_ref=recv.at[origin], send_sem=bulk_send, recv_sem=bulk_recv.at[origin],
            device_id={"shot": g}, device_id_type=MESH)

    def halo_copy(g):
        return pltpu.make_async_remote_copy(
            src_ref=halo_out.at[g * per_owner // per_pack], dst_ref=halo_in.at[group], send_sem=halo_send,
            recv_sem=halo_recv, device_id={"shot": g}, device_id_type=MESH)

    for g in range(min(EARLY, groups)):
        @pl.when(g < group)
        def _():
            bulk(g, group).start()

    @pl.when(depth > 0)
    def _():
        edge_copy(0).wait_send()
        edge_copy(1).wait_recv()

    @pl.when(depth < slabs - 1)
    def _():
        edge_copy(1).wait_send()
        edge_copy(0).wait_recv()

    lane_shot = lax.rem(lane // (2 * tiles), shots)
    for p in range(packs):
        halo = jnp.where(lane % 2 == 0, pltpu.roll(edge_in[1, p], LANES - 1, 1), pltpu.roll(edge_in[0, p], 1, 1))
        halo_out[p] = halo
        change = halo * (halo - 2.0 * packed[p])
        for s in range(shots):
            energies[s] = energies[s] + jnp.where(lane_shot == s, change, 0.0)

    def total(value):
        return jnp.sum(jnp.sum(value, axis=0, keepdims=True), axis=1, keepdims=True)

    note = jnp.zeros((1, LANES), jnp.float32)
    gap = LANES // shots
    lane_row = lax.broadcasted_iota(jnp.int32, (1, LANES), 1)
    for s in range(shots):
        note = jnp.where(lane_row // gap == s, total(energies[s]), note)
    message[pl.ds(0, 1)] = note / cells

    slot = depth * groups + group
    own_note = pltpu.make_async_copy(message.at[pl.ds(0, 1)], inbox.at[pl.ds(slot, 1)], note_recv)
    own_note.start()

    def tell(g, d):
        pltpu.make_async_remote_copy(
            src_ref=message.at[pl.ds(0, 1)], dst_ref=inbox.at[pl.ds(slot, 1)], send_sem=note_send, recv_sem=note_recv,
            device_id={"shot": g, "depth": d}, device_id_type=MESH).start()

    pl.semaphore_wait(passed, slabs - 1)
    for g in range(groups):
        @pl.when(g < group)
        def _():
            for d in range(slabs):
                tell(g, d)
    for d in range(slabs):
        @pl.when(d != depth)
        def _():
            tell(group, d)
    for g in range(groups):
        @pl.when(g < group)
        def _():
            halo_copy(g).start()
    for g in range(EARLY, groups):
        @pl.when(g < group)
        def _():
            bulk(g, group).start()
    for g in range(1, groups):
        @pl.when(g > group)
        def _():
            pl.semaphore_wait(ready.at[g], 1)
            bulk(g, group).start()
            halo_copy(g).start()
            for d in range(slabs):
                tell(g, d)

    recv[group] = send[group]
    halo_in[group] = halo_out[lax.div(group * per_owner, per_pack)]

    col = [(sub + t * SUBLANES).astype(jnp.float32) for t in range(2 * tiles)]
    for g in range(groups):
        @pl.when(g != group)
        def _():
            bulk(g, g).wait_recv()

        for s in range(shots):
            first = recv[g, pl.ds(placed + s, 1)]
            masks = []
            for t in range(2 * tiles):
                offset = col[t] - first
                masks.append((offset == -1.0, offset == float(half), (offset >= -1.0) & (offset <= float(half))))
            for i in range(owned):
                index = s * owned + i
                low = recv[g, pl.ds(border + 2 * s * owned + i, 1)]
                high = recv[g, pl.ds(border + (2 * s + 1) * owned + i, 1)]
                for t in range(2 * tiles):
                    at_low, at_high, inside = masks[t]
                    value = recv[g, pl.ds(index * half + (t % tiles) * SUBLANES, SUBLANES)]
                    value = jnp.where(at_low, low, jnp.where(at_high, high, value))
                    spread[g, s, i, pl.ds(t * SUBLANES, SUBLANES)] = jnp.where(inside, value, 0.0)

    arrived = halo_in.at[pl.ds(0, groups - 1)]
    pltpu.make_async_copy(arrived, arrived, halo_recv).wait()
    fold_col = (lax.rem(lane // 2, tiles) * SUBLANES + sub).astype(jnp.float32)
    for g in range(groups):
        first = recv[g, pl.ds(placed, 1)]
        for s in range(1, shots):
            first = jnp.where(lane_shot == s, recv[g, pl.ds(placed + s, 1)], first)
        halo = halo_in[g]
        halves[g, 0] = jnp.where(fold_col >= first, halo, 0.0)
        halves[g, 1] = jnp.where(fold_col >= first, 0.0, halo)

    pltpu.make_async_copy(inbox, inbox, note_recv).wait()
    meansq = inbox[pl.ds(0, groups)]
    for d in range(1, slabs):
        meansq = meansq + inbox[pl.ds(d * groups, groups)]
    lane_group = lax.broadcasted_iota(jnp.int32, (groups, LANES), 1) // gap
    turned = [meansq] + [pltpu.roll(meansq, j * gap, 1) for j in range(1, shots)]
    by_shot = []
    for s in range(shots):
        value = meansq
        for j in range(1, shots):
            value = jnp.where(lane_group == (s + j) % shots, turned[j], value)
        by_shot.append(value)
    peak = by_shot[0]
    for s in range(1, shots):
        peak = jnp.maximum(peak, by_shot[s])
    peak = 0.5 * jnp.max(peak, axis=0, keepdims=True) + 1.0
    factors = [(1.0 / math.sqrt(shots * groups)) / jnp.sqrt(by_shot[s] + peak) for s in range(shots)]
    factor = factors[0]
    lane_row_shot = lax.rem(lax.broadcasted_iota(jnp.int32, (groups, LANES), 1) // (2 * tiles), shots)
    for s in range(1, shots):
        factor = jnp.where(lane_row_shot == s, factors[s], factor)
    sums = [[zero] * (2 * tiles) for i in range(owned)]
    for h in range(2):
        halo = zero
        for g in range(groups):
            halo = halo + factor[g:g + 1] * halves[g, h]
        origin = 2 * lax.rem(group * per_owner, per_pack) + 1
        for i in range(owned):
            for t in range(tiles):
                value = zero
                for s in range(shots):
                    place = origin + 2 * ((i * shots + s) * tiles + t)
                    value = value + pltpu.roll(halo, 2 * LANES - place, 1)
                ends = (lane == 0) | (lane == LANES - 1)
                sums[i][h * tiles + t] = jnp.where(ends, 0.0 - value, 0.0)
    for s in range(shots):
        for g in range(groups):
            for i in range(owned):
                for t in range(2 * tiles):
                    sums[i][t] = sums[i][t] + factors[s][g:g + 1] * spread[g, s, i, pl.ds(t * SUBLANES, SUBLANES)]
    for i in range(owned):
        for t in range(2 * tiles):
            out_ref[i, pl.ds(t * SUBLANES, SUBLANES)] = sums[i][t]

    pltpu.make_async_copy(inbox.at[pl.ds(0, devices - 1)], inbox.at[pl.ds(0, devices - 1)], note_send).wait()
    pltpu.make_async_copy(arrived, arrived, halo_send).wait()
    others = send.at[pl.ds(0, groups - 1)]
    pltpu.make_async_copy(others, others, bulk_send).wait()


def on_device(correlation, illumination, aperture):
    shots, rows, cols, slab = correlation.shape
    groups = lax.axis_size("shot")
    slabs = lax.axis_size("depth")
    owned = rows // groups
    half = cols // 2
    tiles = half // SUBLANES
    dims = (shots, rows, cols, slab, groups, slabs, owned, rows * cols * slab * slabs)
    packs = -(-rows * shots * tiles // (LANES // 2))
    block = (shots * owned * (half + 2) + shots, slab)
    f32 = jnp.float32
    dma = pltpu.SemaphoreType.DMA
    regular = pltpu.SemaphoreType.REGULAR
    return pl.pallas_call(
        functools.partial(kernel, dims),
        out_shape=pltpu.VMEM((owned, cols, slab), f32),
        in_specs=[pl.BlockSpec(memory_space=pl.ANY)] * 3,
        out_specs=pl.BlockSpec(memory_space=pltpu.VMEM),
        scratch_shapes=[
            pltpu.SMEM(aperture.shape, jnp.int32),
            pltpu.VMEM((2, shots, rows, cols, slab), f32),
            pltpu.VMEM((shots, rows + 2, half + 2 * SUBLANES, slab), f32),
            pltpu.VMEM((shots, rows, half, slab), f32),
            pltpu.VMEM((packs, SUBLANES, LANES), f32),
            pltpu.VMEM((2, packs, SUBLANES, LANES), f32),
            pltpu.VMEM((packs, SUBLANES, LANES), f32),
            pltpu.VMEM((groups, SUBLANES, LANES), f32),
            pltpu.VMEM((groups, 2, SUBLANES, LANES), f32),
            pltpu.VMEM((groups,) + block, f32),
            pltpu.VMEM((groups,) + block, f32),
            pltpu.VMEM((SUBLANES, LANES), f32),
            pltpu.VMEM((slabs * groups, LANES), f32),
            pltpu.VMEM((groups, shots, owned, cols, slab), f32),
            dma,
            dma,
            regular((groups,)),
            regular,
            dma((2,)),
            dma((2,)),
            dma,
            dma((groups,)),
            dma,
            dma,
            dma,
            dma,
        ],
        compiler_params=pltpu.CompilerParams(collective_id=0, has_side_effects=True),
    )(correlation, illumination, aperture)


def solution(mesh):
    return jax.shard_map(
        on_device,
        mesh=mesh,
        in_specs=(P("shot", None, None, "depth"), P("shot", None, None, "depth"), P("shot", None)),
        out_specs=P("shot", None, "depth"),
        check_vma=False,
    )
```

time: 15.9 us -> 14.6 us (0.918)
  the two profiles are of different devices: /device:TPU:13 before, /device:TPU:25 now
where the time goes in v2:
time: 14.6 us; the launch traced here: 14.4 us
  Pallas kernels  13.8 us (95%)
  local copies, waits for them, and re-layouts  0.62 us (4%)
    pallas_call x1, Pallas kernels, on_device(): pl.pallas_call(functools.partial(kernel, dims), out_shape=pltpu.VMEM((own...  13.8 us
    unnamed x1, local copies, waits for them, and re-layouts  0.62 us

profile of v2, /device:TPU:25, one launch (start us, length us, event | category | flops | bytes accessed | tf_op | source)
XLA Modules:
  0.0 14.4 jit_solution(13874654156863047564)
XLA Ops:
  0.0 13.8 %shard_map.37 = f32[2,32,128]{2,1,0:T(8,128)S(1)} custom-call(f32[2,16,32,128]{3,2,1,0:T(8,128)} %corr_hbm.1, f32[2,16,32,128]{3,2,1,0:T(8,128)} %ill_hbm.1, s32[2,4]{1,0:T(2,128)} %box_hbm.1), custom_call_target="tpu_custom_call" | custom-call | tf_op jit(solution)/shard_map/pallas_call | solution.py:336
  13.8 0.6 %copy.5 = f32[2,32,128]{2,1,0:T(8,128)} copy(f32[2,32,128]{2,1,0:T(8,128)S(1)} %shard_map.37) | data formatting | bytes 65536

commit v3 on v2

--- a/solution.py
+++ b/solution.py
@@ -162,10 +162,11 @@
 
     def halo_copy(g):
         return pltpu.make_async_remote_copy(
-            src_ref=halo_out.at[g * per_owner // per_pack], dst_ref=halo_in.at[group], send_sem=halo_send,
+            src_ref=halo_out.at[g * per_owner // per_pack], dst_ref=halo_in.at[group], send_sem=halo_send.at[g],
             recv_sem=halo_recv, device_id={"shot": g}, device_id_type=MESH)
 
-    for g in range(min(EARLY, groups)):
+    early = min(EARLY, groups)
+    for g in range(early):
         @pl.when(g < group)
         def _():
             bulk(g, group).start()
@@ -181,9 +182,11 @@
         edge_copy(0).wait_recv()
 
     lane_shot = lax.rem(lane // (2 * tiles), shots)
+    halos = []
     for p in range(packs):
         halo = jnp.where(lane % 2 == 0, pltpu.roll(edge_in[1, p], LANES - 1, 1), pltpu.roll(edge_in[0, p], 1, 1))
         halo_out[p] = halo
+        halos.append(halo)
         change = halo * (halo - 2.0 * packed[p])
         for s in range(shots):
             energies[s] = energies[s] + jnp.where(lane_shot == s, change, 0.0)
@@ -217,25 +220,32 @@
         @pl.when(d != depth)
         def _():
             tell(group, d)
-    for g in range(groups):
+    for g in range(early):
         @pl.when(g < group)
         def _():
             halo_copy(g).start()
-    for g in range(EARLY, groups):
+    ends = (lane == 0) | (lane == LANES - 1)
+    for owner in range(early, groups):
+        for i in range(owned):
+            for s in range(shots):
+                for t in range(tiles):
+                    p, k = lane_of(owner * owned + i, s, t)
+                    here = pl.ds((s * owned + i) * half + t * SUBLANES, SUBLANES)
+                    moved = pltpu.roll(halos[p], LANES - 1 - k, 1)
+                    send[owner, here] = send[owner, here] - jnp.where(ends, moved, 0.0)
+    for g in range(early, groups):
         @pl.when(g < group)
         def _():
             bulk(g, group).start()
-    for g in range(1, groups):
+    for g in sorted(range(1, groups), key=lambda g: (g % 2, g) if 2 * g >= groups else (0, 0)):
         @pl.when(g > group)
         def _():
             pl.semaphore_wait(ready.at[g], 1)
             bulk(g, group).start()
-            halo_copy(g).start()
             for d in range(slabs):
                 tell(g, d)
 
     recv[group] = send[group]
-    halo_in[group] = halo_out[lax.div(group * per_owner, per_pack)]
 
     col = [(sub + t * SUBLANES).astype(jnp.float32) for t in range(2 * tiles)]
     for g in range(groups):
@@ -260,15 +270,19 @@
                     spread[g, s, i, pl.ds(t * SUBLANES, SUBLANES)] = jnp.where(inside, value, 0.0)
 
     arrived = halo_in.at[pl.ds(0, groups - 1)]
-    pltpu.make_async_copy(arrived, arrived, halo_recv).wait()
-    fold_col = (lax.rem(lane // 2, tiles) * SUBLANES + sub).astype(jnp.float32)
-    for g in range(groups):
-        first = recv[g, pl.ds(placed, 1)]
-        for s in range(1, shots):
-            first = jnp.where(lane_shot == s, recv[g, pl.ds(placed + s, 1)], first)
-        halo = halo_in[g]
-        halves[g, 0] = jnp.where(fold_col >= first, halo, 0.0)
-        halves[g, 1] = jnp.where(fold_col >= first, 0.0, halo)
+
+    @pl.when(group < early)
+    def _():
+        halo_in[group] = halo_out[lax.div(group * per_owner, per_pack)]
+        pltpu.make_async_copy(arrived, arrived, halo_recv).wait()
+        fold_col = (lax.rem(lane // 2, tiles) * SUBLANES + sub).astype(jnp.float32)
+        for g in range(groups):
+            first = recv[g, pl.ds(placed, 1)]
+            for s in range(1, shots):
+                first = jnp.where(lane_shot == s, recv[g, pl.ds(placed + s, 1)], first)
+            halo = halo_in[g]
+            halves[g, 0] = jnp.where(fold_col >= first, halo, 0.0)
+            halves[g, 1] = jnp.where(fold_col >= first, 0.0, halo)
 
     pltpu.make_async_copy(inbox, inbox, note_recv).wait()
     meansq = inbox[pl.ds(0, groups)]
@@ -287,35 +301,42 @@
         peak = jnp.maximum(peak, by_shot[s])
     peak = 0.5 * jnp.max(peak, axis=0, keepdims=True) + 1.0
     factors = [(1.0 / math.sqrt(shots * groups)) / jnp.sqrt(by_shot[s] + peak) for s in range(shots)]
-    factor = factors[0]
-    lane_row_shot = lax.rem(lax.broadcasted_iota(jnp.int32, (groups, LANES), 1) // (2 * tiles), shots)
-    for s in range(1, shots):
-        factor = jnp.where(lane_row_shot == s, factors[s], factor)
-    sums = [[zero] * (2 * tiles) for i in range(owned)]
-    for h in range(2):
-        halo = zero
-        for g in range(groups):
-            halo = halo + factor[g:g + 1] * halves[g, h]
-        origin = 2 * lax.rem(group * per_owner, per_pack) + 1
-        for i in range(owned):
-            for t in range(tiles):
-                value = zero
-                for s in range(shots):
-                    place = origin + 2 * ((i * shots + s) * tiles + t)
-                    value = value + pltpu.roll(halo, 2 * LANES - place, 1)
-                ends = (lane == 0) | (lane == LANES - 1)
-                sums[i][h * tiles + t] = jnp.where(ends, 0.0 - value, 0.0)
-    for s in range(shots):
-        for g in range(groups):
-            for i in range(owned):
-                for t in range(2 * tiles):
-                    sums[i][t] = sums[i][t] + factors[s][g:g + 1] * spread[g, s, i, pl.ds(t * SUBLANES, SUBLANES)]
     for i in range(owned):
         for t in range(2 * tiles):
-            out_ref[i, pl.ds(t * SUBLANES, SUBLANES)] = sums[i][t]
+            total_t = None
+            for s in range(shots):
+                part = factors[s][0:1] * spread[0, s, i, pl.ds(t * SUBLANES, SUBLANES)]
+                for g in range(1, groups):
+                    part = part + factors[s][g:g + 1] * spread[g, s, i, pl.ds(t * SUBLANES, SUBLANES)]
+                total_t = part if total_t is None else total_t + part
+            out_ref[i, pl.ds(t * SUBLANES, SUBLANES)] = total_t
+
+    @pl.when(group < early)
+    def _():
+        factor = factors[0]
+        lane_row_shot = lax.rem(lax.broadcasted_iota(jnp.int32, (groups, LANES), 1) // (2 * tiles), shots)
+        for s in range(1, shots):
+            factor = jnp.where(lane_row_shot == s, factors[s], factor)
+        origin = 2 * lax.rem(group * per_owner, per_pack) + 1
+        for h in range(2):
+            halo = factor[0:1] * halves[0, h]
+            for g in range(1, groups):
+                halo = halo + factor[g:g + 1] * halves[g, h]
+            for i in range(owned):
+                for t in range(tiles):
+                    value = None
+                    for s in range(shots):
+                        shift = 2 * LANES - origin - 2 * ((i * shots + s) * tiles + t)
+                        moved = pltpu.roll(halo, shift, 1)
+                        value = moved if value is None else value + moved
+                    here = pl.ds((h * tiles + t) * SUBLANES, SUBLANES)
+                    out_ref[i, here] = out_ref[i, here] - jnp.where(ends, value, 0.0)
 
     pltpu.make_async_copy(inbox.at[pl.ds(0, devices - 1)], inbox.at[pl.ds(0, devices - 1)], note_send).wait()
-    pltpu.make_async_copy(arrived, arrived, halo_send).wait()
+    for g in range(early):
+        @pl.when(g < group)
+        def _():
+            halo_copy(g).wait_send()
     others = send.at[pl.ds(0, groups - 1)]
     pltpu.make_async_copy(others, others, bulk_send).wait()
 
@@ -361,7 +382,7 @@
             dma((2,)),
             dma,
             dma((groups,)),
-            dma,
+            dma((min(EARLY, groups),)),
             dma,
             dma,
             dma,

time: 14.6 us -> 13.8 us (0.945)
  the two profiles are of different devices: /device:TPU:25 before, /device:TPU:29 now
where the time goes in v3:
time: 13.8 us; the launch traced here: 13.7 us
  Pallas kernels  13 us (94%)
  local copies, waits for them, and re-layouts  0.62 us (4%)
    pallas_call x1, Pallas kernels, on_device(): pl.pallas_call(functools.partial(kernel, dims), out_shape=pltpu.VMEM((own...  13 us
    unnamed x1, local copies, waits for them, and re-layouts  0.62 us

profile of v3, /device:TPU:29, one launch (start us, length us, event | category | flops | bytes accessed | tf_op | source)
XLA Modules:
  0.0 13.7 jit_solution(16532097753530723224)
XLA Ops:
  0.0 13.0 %shard_map.37 = f32[2,32,128]{2,1,0:T(8,128)S(1)} custom-call(f32[2,16,32,128]{3,2,1,0:T(8,128)} %corr_hbm.1, f32[2,16,32,128]{3,2,1,0:T(8,128)} %ill_hbm.1, s32[2,4]{1,0:T(2,128)} %box_hbm.1), custom_call_target="tpu_custom_call" | custom-call | tf_op jit(solution)/shard_map/pallas_call | solution.py:357
  13.0 0.6 %copy.5 = f32[2,32,128]{2,1,0:T(8,128)} copy(f32[2,32,128]{2,1,0:T(8,128)S(1)} %shard_map.37) | data formatting | bytes 65536

commit v4 on v3

--- a/solution.py
+++ b/solution.py
@@ -15,7 +15,7 @@
 
 
 def kernel(dims, corr_hbm, ill_hbm, box_hbm, out_ref, box, raw, norm, centre, edge_out, edge_in, halo_out, halo_in, halves, send, recv, message, inbox, spread,
-           load_sem, box_sem, ready, passed, edge_send, edge_recv, bulk_send, bulk_recv, halo_send, halo_recv, note_send, note_recv):
+           ready, passed, edge_send, edge_recv, bulk_send, bulk_recv, halo_recv, note_send, note_recv):
     shots, rows, cols, slab, groups, slabs, owned, cells = dims
     half = cols // 2
     tiles = half // SUBLANES
@@ -28,11 +28,11 @@
     placed = border + 2 * shots * owned
     corr, ill = raw.at[0], raw.at[1]
 
-    box_copy = pltpu.make_async_copy(box_hbm, box, box_sem)
+    box_copy = pltpu.make_async_copy(box_hbm, box, bulk_send)
     box_copy.start()
     for s in range(shots):
         for source, target in ((corr_hbm, corr), (ill_hbm, ill)):
-            pltpu.make_async_copy(source.at[s], target.at[s], load_sem).start()
+            pltpu.make_async_copy(source.at[s], target.at[s], note_send).start()
 
     def signal(semaphore, **device):
         pl.semaphore_signal(semaphore, inc=1, device_id=device, device_id_type=MESH)
@@ -72,7 +72,48 @@
         start.append(jnp.minimum(first, half))
         lower.append([(sub + t * SUBLANES >= first) & (sub + t * SUBLANES < last) for t in range(tiles)])
         upper.append([(sub + t * SUBLANES + half >= first) & (sub + t * SUBLANES + half < last) for t in range(tiles)])
-    pltpu.make_async_copy(raw, raw, load_sem).wait()
+    pltpu.make_async_copy(raw, raw, note_send).wait()
+
+    def lane_of(r, s, t):
+        k = (r * shots + s) * tiles + t
+        return k // per_pack, 2 * (k % per_pack)
+
+    packed = [zero] * packs
+    for r in range(rows):
+        for s in range(shots):
+            in_row = (r >= box[s, 0]) & (r < box[s, 1])
+            parts = []
+            for t in range(tiles):
+                here = pl.ds(t * SUBLANES, SUBLANES)
+                there = pl.ds(t * SUBLANES + half, SUBLANES)
+                top = jnp.where(upper[s][t], corr[s, r, there], corr[s, r, here])
+                top = jnp.where((lower[s][t] | upper[s][t]) & in_row, top, 0.0)
+                value = top / (jnp.where(upper[s][t], ill[s, r, there], ill[s, r, here]) + 0.1)
+                parts.append(value)
+                p, k = lane_of(r, s, t)
+                packed[p] = jnp.where(lane // 2 == k // 2, pltpu.roll(value, k + 1, 1), packed[p])
+            for t, value in enumerate([parts[-1]] + parts + [parts[0]]):
+                norm[s, r + 1, pl.ds(t * SUBLANES, SUBLANES)] = value
+    for p in range(packs):
+        edge_out[p] = packed[p]
+
+    def edge_copy(side):
+        return pltpu.make_async_remote_copy(
+            src_ref=edge_out, dst_ref=edge_in.at[1 - side], send_sem=edge_send,
+            recv_sem=edge_recv, device_id={"depth": depth + (1 if side else -1)}, device_id_type=MESH)
+
+    pl.semaphore_wait(barrier, group + slabs - 1)
+
+    @pl.when(depth > 0)
+    def _():
+        edge_copy(0).start()
+
+    @pl.when(depth < slabs - 1)
+    def _():
+        edge_copy(1).start()
+
+    each(0, group, lambda g: signal(ready.at[group - 1], shot=g))
+    each(1, slabs, lambda d: signal(passed, depth=lax.rem(depth + d, slabs)))
 
     row_index = lax.broadcasted_iota(jnp.int32, (rows, slab), 0)
     energies = []
@@ -94,49 +135,13 @@
         for owner in range(groups):
             send[owner, pl.ds(placed + s, 1)] = jnp.full((1, LANES), start[s].astype(jnp.float32))
 
-    def lane_of(r, s, t):
-        k = (r * shots + s) * tiles + t
-        return k // per_pack, 2 * (k % per_pack)
-
-    packed = [zero] * packs
     for r in range(rows):
         for s in range(shots):
-            in_row = (r >= box[s, 0]) & (r < box[s, 1])
-            parts = []
             for t in range(tiles):
-                here = pl.ds(t * SUBLANES, SUBLANES)
-                there = pl.ds(t * SUBLANES + half, SUBLANES)
-                top = jnp.where(upper[s][t], corr[s, r, there], corr[s, r, here])
-                top = jnp.where((lower[s][t] | upper[s][t]) & in_row, top, 0.0)
-                value = top / (jnp.where(upper[s][t], ill[s, r, there], ill[s, r, here]) + 0.1)
-                parts.append(value)
-                p, k = lane_of(r, s, t)
-                packed[p] = jnp.where(lane // 2 == k // 2, pltpu.roll(value, k + 1, 1), packed[p])
+                value = norm[s, r + 1, pl.ds((t + 1) * SUBLANES, SUBLANES)]
                 beside = jnp.where(lane > 0, pltpu.roll(value, 1, 1), 0.0)
                 beside = beside + jnp.where(lane < LANES - 1, pltpu.roll(value, LANES - 1, 1), 0.0)
                 centre[s, r, pl.ds(t * SUBLANES, SUBLANES)] = 6.0 * value - beside
-            for t, value in enumerate([parts[-1]] + parts + [parts[0]]):
-                norm[s, r + 1, pl.ds(t * SUBLANES, SUBLANES)] = value
-    for p in range(packs):
-        edge_out[p] = packed[p]
-
-    def edge_copy(side):
-        return pltpu.make_async_remote_copy(
-            src_ref=edge_out, dst_ref=edge_in.at[1 - side], send_sem=edge_send.at[side],
-            recv_sem=edge_recv.at[1 - side], device_id={"depth": depth + (1 if side else -1)}, device_id_type=MESH)
-
-    pl.semaphore_wait(barrier, group + slabs - 1)
-
-    @pl.when(depth > 0)
-    def _():
-        edge_copy(0).start()
-
-    @pl.when(depth < slabs - 1)
-    def _():
-        edge_copy(1).start()
-
-    each(0, group, lambda g: signal(ready.at[group], shot=g))
-    each(1, slabs, lambda d: signal(passed, depth=lax.rem(depth + d, slabs)))
 
     no_before = [[sub + t * SUBLANES == lax.rem(start[s], half) for t in range(tiles)] for s in range(shots)]
     no_after = [[sub + t * SUBLANES == lax.rem(start[s] + half - 1, half) for t in range(tiles)] for s in range(shots)]
@@ -157,12 +162,12 @@
 
     def bulk(g, origin):
         return pltpu.make_async_remote_copy(
-            src_ref=send.at[g], dst_ref=recv.at[origin], send_sem=bulk_send, recv_sem=bulk_recv.at[origin],
+            src_ref=send.at[g], dst_ref=recv.at[origin], send_sem=bulk_send, recv_sem=bulk_recv.at[lax.div(origin, 2)],
             device_id={"shot": g}, device_id_type=MESH)
 
     def halo_copy(g):
         return pltpu.make_async_remote_copy(
-            src_ref=halo_out.at[g * per_owner // per_pack], dst_ref=halo_in.at[group], send_sem=halo_send.at[g],
+            src_ref=halo_out.at[g * per_owner // per_pack], dst_ref=halo_in.at[group], send_sem=edge_send,
             recv_sem=halo_recv, device_id={"shot": g}, device_id_type=MESH)
 
     early = min(EARLY, groups)
@@ -171,15 +176,12 @@
         def _():
             bulk(g, group).start()
 
-    @pl.when(depth > 0)
-    def _():
-        edge_copy(0).wait_send()
-        edge_copy(1).wait_recv()
-
-    @pl.when(depth < slabs - 1)
-    def _():
-        edge_copy(1).wait_send()
-        edge_copy(0).wait_recv()
+    for inner, count in ((True, 2), (False, 1)):
+        @pl.when(((depth > 0) & (depth < slabs - 1)) == inner)
+        def _():
+            tile = edge_in.at[pl.ds(0, count)]
+            pltpu.make_async_copy(tile, tile, edge_send).wait()
+            pltpu.make_async_copy(tile, tile, edge_recv).wait()
 
     lane_shot = lax.rem(lane // (2 * tiles), shots)
     halos = []
@@ -191,39 +193,6 @@
         for s in range(shots):
             energies[s] = energies[s] + jnp.where(lane_shot == s, change, 0.0)
 
-    def total(value):
-        return jnp.sum(jnp.sum(value, axis=0, keepdims=True), axis=1, keepdims=True)
-
-    note = jnp.zeros((1, LANES), jnp.float32)
-    gap = LANES // shots
-    lane_row = lax.broadcasted_iota(jnp.int32, (1, LANES), 1)
-    for s in range(shots):
-        note = jnp.where(lane_row // gap == s, total(energies[s]), note)
-    message[pl.ds(0, 1)] = note / cells
-
-    slot = depth * groups + group
-    own_note = pltpu.make_async_copy(message.at[pl.ds(0, 1)], inbox.at[pl.ds(slot, 1)], note_recv)
-    own_note.start()
-
-    def tell(g, d):
-        pltpu.make_async_remote_copy(
-            src_ref=message.at[pl.ds(0, 1)], dst_ref=inbox.at[pl.ds(slot, 1)], send_sem=note_send, recv_sem=note_recv,
-            device_id={"shot": g, "depth": d}, device_id_type=MESH).start()
-
-    pl.semaphore_wait(passed, slabs - 1)
-    for g in range(groups):
-        @pl.when(g < group)
-        def _():
-            for d in range(slabs):
-                tell(g, d)
-    for d in range(slabs):
-        @pl.when(d != depth)
-        def _():
-            tell(group, d)
-    for g in range(early):
-        @pl.when(g < group)
-        def _():
-            halo_copy(g).start()
     ends = (lane == 0) | (lane == LANES - 1)
     for owner in range(early, groups):
         for i in range(owned):
@@ -233,14 +202,48 @@
                     here = pl.ds((s * owned + i) * half + t * SUBLANES, SUBLANES)
                     moved = pltpu.roll(halos[p], LANES - 1 - k, 1)
                     send[owner, here] = send[owner, here] - jnp.where(ends, moved, 0.0)
+
+    def total(value):
+        return jnp.sum(jnp.sum(value, axis=0, keepdims=True), axis=1, keepdims=True)
+
+    note = jnp.zeros((1, LANES), jnp.float32)
+    gap = LANES // shots
+    lane_row = lax.broadcasted_iota(jnp.int32, (1, LANES), 1)
+    for s in range(shots):
+        note = jnp.where(lane_row // gap == s, total(energies[s]), note)
+    message[pl.ds(0, 1)] = note / cells
+
+    slot = depth * groups + group
+    own_note = pltpu.make_async_copy(message.at[pl.ds(0, 1)], inbox.at[pl.ds(slot, 1)], note_recv)
+    own_note.start()
+
+    def tell(g, d):
+        pltpu.make_async_remote_copy(
+            src_ref=message.at[pl.ds(0, 1)], dst_ref=inbox.at[pl.ds(slot, 1)], send_sem=note_send, recv_sem=note_recv,
+            device_id={"shot": g, "depth": d}, device_id_type=MESH).start()
+
+    pl.semaphore_wait(passed, slabs - 1)
+    for g in range(groups):
+        @pl.when(g < group)
+        def _():
+            for d in range(slabs):
+                tell(g, d)
+    for d in range(slabs):
+        @pl.when(d != depth)
+        def _():
+            tell(group, d)
+    for g in range(early):
+        @pl.when(g < group)
+        def _():
+            halo_copy(g).start()
     for g in range(early, groups):
         @pl.when(g < group)
         def _():
             bulk(g, group).start()
-    for g in sorted(range(1, groups), key=lambda g: (g % 2, g) if 2 * g >= groups else (0, 0)):
+    for g in sorted(range(1, groups), key=lambda g: (g % 2, g) if 2 * g >= groups else (2, g)):
         @pl.when(g > group)
         def _():
-            pl.semaphore_wait(ready.at[g], 1)
+            pl.semaphore_wait(ready.at[g - 1], 1)
             bulk(g, group).start()
             for d in range(slabs):
                 tell(g, d)
@@ -249,9 +252,12 @@
 
     col = [(sub + t * SUBLANES).astype(jnp.float32) for t in range(2 * tiles)]
     for g in range(groups):
-        @pl.when(g != group)
-        def _():
-            bulk(g, g).wait_recv()
+        if g % 2 == 0:
+            for own, count in ((True, 1), (False, 2)):
+                @pl.when((lax.div(group, 2) == g // 2) == own)
+                def _():
+                    pair = recv.at[pl.ds(g, count)]
+                    pltpu.make_async_copy(pair, pair, bulk_recv.at[g // 2]).wait()
 
         for s in range(shots):
             first = recv[g, pl.ds(placed + s, 1)]
@@ -334,9 +340,11 @@
 
     pltpu.make_async_copy(inbox.at[pl.ds(0, devices - 1)], inbox.at[pl.ds(0, devices - 1)], note_send).wait()
     for g in range(early):
-        @pl.when(g < group)
-        def _():
-            halo_copy(g).wait_send()
+        sent = min(g + 1, early)
+
+        @pl.when((group == g + 1) if g + 1 < early else (group > g))
+        def _():
+            pltpu.make_async_copy(halo_in.at[pl.ds(0, sent)], halo_in.at[pl.ds(0, sent)], edge_send).wait()
     others = send.at[pl.ds(0, groups - 1)]
     pltpu.make_async_copy(others, others, bulk_send).wait()
 
@@ -374,15 +382,12 @@
             pltpu.VMEM((SUBLANES, LANES), f32),
             pltpu.VMEM((slabs * groups, LANES), f32),
             pltpu.VMEM((groups, shots, owned, cols, slab), f32),
-            dma,
-            dma,
-            regular((groups,)),
+            regular((groups - 1,)),
             regular,
-            dma((2,)),
-            dma((2,)),
-            dma,
-            dma((groups,)),
-            dma((min(EARLY, groups),)),
+            dma,
+            dma,
+            dma,
+            dma((groups // 2,)),
             dma,
             dma,
             dma,

time: 13.8 us -> 13.4 us (0.971)
  Pallas kernels: 13 us -> 12.6 us
    pallas_call x1, Pallas kernels: 13 us -> 12.6 us  [on_device(): pl.pallas_call(functools.partial(kernel, dims), out_shape=pltpu.VMEM((own...]
where the time goes in v4:
time: 13.4 us; the launch traced here: 13.2 us
  Pallas kernels  12.6 us (94%)
  local copies, waits for them, and re-layouts  0.62 us (5%)
    pallas_call x1, Pallas kernels, on_device(): pl.pallas_call(functools.partial(kernel, dims), out_shape=pltpu.VMEM((own...  12.6 us
    unnamed x1, local copies, waits for them, and re-layouts  0.62 us

profile of v4, /device:TPU:29, one launch (start us, length us, event | category | flops | bytes accessed | tf_op | source)
XLA Modules:
  0.0 13.2 jit_solution(11670184063065635467)
XLA Ops:
  0.0 12.6 %shard_map.37 = f32[2,32,128]{2,1,0:T(8,128)S(1)} custom-call(f32[2,16,32,128]{3,2,1,0:T(8,128)} %corr_hbm.1, f32[2,16,32,128]{3,2,1,0:T(8,128)} %ill_hbm.1, s32[2,4]{1,0:T(2,128)} %box_hbm.1), custom_call_target="tpu_custom_call" | custom-call | tf_op jit(solution)/shard_map/pallas_call | solution.py:365
  12.6 0.6 %copy.5 = f32[2,32,128]{2,1,0:T(8,128)} copy(f32[2,32,128]{2,1,0:T(8,128)S(1)} %shard_map.37) | data formatting | bytes 65536

commit v5 on v4

--- a/solution.py
+++ b/solution.py
@@ -14,7 +14,7 @@
 EARLY = 1
 
 
-def kernel(dims, corr_hbm, ill_hbm, box_hbm, out_ref, box, raw, norm, centre, edge_out, edge_in, halo_out, halo_in, halves, send, recv, message, inbox, spread,
+def kernel(dims, corr_hbm, ill_hbm, box_hbm, out_ref, box, raw, norm, centre, edge_out, edge_in, halo_out, halo_in, halves, spare, send, recv, message, inbox, spread,
            ready, passed, edge_send, edge_recv, bulk_send, bulk_recv, halo_recv, note_send, note_recv):
     shots, rows, cols, slab, groups, slabs, owned, cells = dims
     half = cols // 2
@@ -102,6 +102,56 @@
             src_ref=edge_out, dst_ref=edge_in.at[1 - side], send_sem=edge_send,
             recv_sem=edge_recv, device_id={"depth": depth + (1 if side else -1)}, device_id_type=MESH)
 
+    def laplacian():
+        row_index = lax.broadcasted_iota(jnp.int32, (rows, slab), 0)
+        energies = []
+        for s in range(shots):
+            in_rows = (row_index >= box[s, 0]) & (row_index < box[s, 1])
+            energy = None
+            for side, column in enumerate((start[s], start[s] + half - 1)):
+                in_box = (column >= box[s, 2]) & (column < box[s, 3])
+                value = jnp.where(in_rows & in_box, corr[s, :, column], 0.0) / (ill[s, :, column] + 0.1)
+                for owner in range(groups):
+                    send[owner, pl.ds(border + (2 * s + side) * owned, owned)] = 0.0 - value[owner * owned:(owner + 1) * owned]
+                in_grid = (start[s] > 0) if side == 0 else (start[s] < cols - half)
+                kept = jnp.where(in_grid, value, 0.0)
+                kept = kept * kept
+                energy = kept if energy is None else energy + kept
+            while energy.shape[0] > SUBLANES:
+                energy = energy[:energy.shape[0] // 2] + energy[energy.shape[0] // 2:]
+            energies.append(energy)
+            for owner in range(groups):
+                send[owner, pl.ds(placed + s, 1)] = jnp.full((1, LANES), start[s].astype(jnp.float32))
+
+        for r in range(rows):
+            for s in range(shots):
+                for t in range(tiles):
+                    value = norm[s, r + 1, pl.ds((t + 1) * SUBLANES, SUBLANES)]
+                    beside = jnp.where(lane > 0, pltpu.roll(value, 1, 1), 0.0)
+                    beside = beside + jnp.where(lane < LANES - 1, pltpu.roll(value, LANES - 1, 1), 0.0)
+                    centre[s, r, pl.ds(t * SUBLANES, SUBLANES)] = 6.0 * value - beside
+
+        no_before = [[sub + t * SUBLANES == lax.rem(start[s], half) for t in range(tiles)] for s in range(shots)]
+        no_after = [[sub + t * SUBLANES == lax.rem(start[s] + half - 1, half) for t in range(tiles)] for s in range(shots)]
+        packed = [zero] * packs
+        for r in range(rows):
+            owner, i = r // owned, r % owned
+            for s in range(shots):
+                for t in range(tiles):
+                    base = SUBLANES + t * SUBLANES
+                    beside = norm[s, r, pl.ds(base, SUBLANES)] + norm[s, r + 2, pl.ds(base, SUBLANES)]
+                    beside = beside + jnp.where(no_before[s][t], 0.0, norm[s, r + 1, pl.ds(base - 1, SUBLANES)])
+                    beside = beside + jnp.where(no_after[s][t], 0.0, norm[s, r + 1, pl.ds(base + 1, SUBLANES)])
+                    p, k = lane_of(r, s, t)
+                    result = centre[s, r, pl.ds(t * SUBLANES, SUBLANES)] - beside
+                    energies[s] = energies[s] + result * result
+                    packed[p] = jnp.where(lane // 2 == k // 2, pltpu.roll(result, k + 1, 1), packed[p])
+                    send[owner, pl.ds((s * owned + i) * half + t * SUBLANES, SUBLANES)] = result
+        return tuple(energies) + tuple(packed)
+
+    late = (lax.rem(depth, 2) == 1) & (depth < slabs - 1)
+    before = lax.cond(late, laplacian, lambda: (zero,) * (shots + packs))
+
     pl.semaphore_wait(barrier, group + slabs - 1)
 
     @pl.when(depth > 0)
@@ -115,50 +165,8 @@
     each(0, group, lambda g: signal(ready.at[group - 1], shot=g))
     each(1, slabs, lambda d: signal(passed, depth=lax.rem(depth + d, slabs)))
 
-    row_index = lax.broadcasted_iota(jnp.int32, (rows, slab), 0)
-    energies = []
-    for s in range(shots):
-        in_rows = (row_index >= box[s, 0]) & (row_index < box[s, 1])
-        energy = None
-        for side, column in enumerate((start[s], start[s] + half - 1)):
-            in_box = (column >= box[s, 2]) & (column < box[s, 3])
-            value = jnp.where(in_rows & in_box, corr[s, :, column], 0.0) / (ill[s, :, column] + 0.1)
-            for owner in range(groups):
-                send[owner, pl.ds(border + (2 * s + side) * owned, owned)] = 0.0 - value[owner * owned:(owner + 1) * owned]
-            in_grid = (start[s] > 0) if side == 0 else (start[s] < cols - half)
-            kept = jnp.where(in_grid, value, 0.0)
-            kept = kept * kept
-            energy = kept if energy is None else energy + kept
-        while energy.shape[0] > SUBLANES:
-            energy = energy[:energy.shape[0] // 2] + energy[energy.shape[0] // 2:]
-        energies.append(energy)
-        for owner in range(groups):
-            send[owner, pl.ds(placed + s, 1)] = jnp.full((1, LANES), start[s].astype(jnp.float32))
-
-    for r in range(rows):
-        for s in range(shots):
-            for t in range(tiles):
-                value = norm[s, r + 1, pl.ds((t + 1) * SUBLANES, SUBLANES)]
-                beside = jnp.where(lane > 0, pltpu.roll(value, 1, 1), 0.0)
-                beside = beside + jnp.where(lane < LANES - 1, pltpu.roll(value, LANES - 1, 1), 0.0)
-                centre[s, r, pl.ds(t * SUBLANES, SUBLANES)] = 6.0 * value - beside
-
-    no_before = [[sub + t * SUBLANES == lax.rem(start[s], half) for t in range(tiles)] for s in range(shots)]
-    no_after = [[sub + t * SUBLANES == lax.rem(start[s] + half - 1, half) for t in range(tiles)] for s in range(shots)]
-    packed = [zero] * packs
-    for r in range(rows):
-        owner, i = r // owned, r % owned
-        for s in range(shots):
-            for t in range(tiles):
-                base = SUBLANES + t * SUBLANES
-                beside = norm[s, r, pl.ds(base, SUBLANES)] + norm[s, r + 2, pl.ds(base, SUBLANES)]
-                beside = beside + jnp.where(no_before[s][t], 0.0, norm[s, r + 1, pl.ds(base - 1, SUBLANES)])
-                beside = beside + jnp.where(no_after[s][t], 0.0, norm[s, r + 1, pl.ds(base + 1, SUBLANES)])
-                p, k = lane_of(r, s, t)
-                result = centre[s, r, pl.ds(t * SUBLANES, SUBLANES)] - beside
-                energies[s] = energies[s] + result * result
-                packed[p] = jnp.where(lane // 2 == k // 2, pltpu.roll(result, k + 1, 1), packed[p])
-                send[owner, pl.ds((s * owned + i) * half + t * SUBLANES, SUBLANES)] = result
+    after = lax.cond(late, lambda: before, laplacian)
+    energies, packed = list(after[:shots]), list(after[shots:])
 
     def bulk(g, origin):
         return pltpu.make_async_remote_copy(
@@ -175,6 +183,20 @@
         @pl.when(g < group)
         def _():
             bulk(g, group).start()
+
+    quarter = groups // 4
+    pairs = ((range(quarter, 2 * quarter), 2 * quarter), (range(2 * quarter, 3 * quarter), quarter))
+    ahead = [late & (group >= sources[0]) & (group <= sources[-1]) for sources, target in pairs]
+    any_ahead = ahead[0] | ahead[1]
+    for here, (sources, target) in zip(ahead, pairs):
+        @pl.when(here)
+        def _():
+            spare[...] = send[target]
+            if target > sources[0]:
+                pl.semaphore_wait(ready.at[target - 1], 1)
+            pltpu.make_async_remote_copy(
+                src_ref=spare, dst_ref=recv.at[group], send_sem=bulk_send, recv_sem=bulk_recv.at[lax.div(group, 2)],
+                device_id={"shot": target}, device_id_type=MESH).start()
 
     for inner, count in ((True, 2), (False, 1)):
         @pl.when(((depth > 0) & (depth < slabs - 1)) == inner)
@@ -236,15 +258,27 @@
         @pl.when(g < group)
         def _():
             halo_copy(g).start()
+
+    for here, (sources, target) in zip(ahead, pairs):
+        @pl.when(here)
+        def _():
+            halo_copy(target).start()
+
     for g in range(early, groups):
-        @pl.when(g < group)
+        @pl.when((g < group) & jnp.logical_not(ahead[1] & (g == pairs[1][1])))
         def _():
             bulk(g, group).start()
     for g in sorted(range(1, groups), key=lambda g: (g % 2, g) if 2 * g >= groups else (2, g)):
         @pl.when(g > group)
         def _():
-            pl.semaphore_wait(ready.at[g - 1], 1)
-            bulk(g, group).start()
+            if g == pairs[0][1]:
+                @pl.when(jnp.logical_not(ahead[0]))
+                def _():
+                    pl.semaphore_wait(ready.at[g - 1], 1)
+                    bulk(g, group).start()
+            else:
+                pl.semaphore_wait(ready.at[g - 1], 1)
+                bulk(g, group).start()
             for d in range(slabs):
                 tell(g, d)
 
@@ -275,20 +309,27 @@
                     value = jnp.where(at_low, low, jnp.where(at_high, high, value))
                     spread[g, s, i, pl.ds(t * SUBLANES, SUBLANES)] = jnp.where(inside, value, 0.0)
 
-    arrived = halo_in.at[pl.ds(0, groups - 1)]
-
-    @pl.when(group < early)
-    def _():
-        halo_in[group] = halo_out[lax.div(group * per_owner, per_pack)]
+    def collect(sources, count):
+        arrived = halo_in.at[pl.ds(0, count)]
         pltpu.make_async_copy(arrived, arrived, halo_recv).wait()
         fold_col = (lax.rem(lane // 2, tiles) * SUBLANES + sub).astype(jnp.float32)
-        for g in range(groups):
+        for g in sources:
             first = recv[g, pl.ds(placed, 1)]
             for s in range(1, shots):
                 first = jnp.where(lane_shot == s, recv[g, pl.ds(placed + s, 1)], first)
             halo = halo_in[g]
             halves[g, 0] = jnp.where(fold_col >= first, halo, 0.0)
             halves[g, 1] = jnp.where(fold_col >= first, 0.0, halo)
+
+    @pl.when(group < early)
+    def _():
+        halo_in[group] = halo_out[lax.div(group * per_owner, per_pack)]
+        collect(range(groups), groups - 1)
+
+    for sources, target in pairs:
+        @pl.when(late & (group == target))
+        def _():
+            collect(sources, len(sources))
 
     pltpu.make_async_copy(inbox, inbox, note_recv).wait()
     meansq = inbox[pl.ds(0, groups)]
@@ -317,16 +358,15 @@
                 total_t = part if total_t is None else total_t + part
             out_ref[i, pl.ds(t * SUBLANES, SUBLANES)] = total_t
 
-    @pl.when(group < early)
-    def _():
+    def correct(sources):
         factor = factors[0]
         lane_row_shot = lax.rem(lax.broadcasted_iota(jnp.int32, (groups, LANES), 1) // (2 * tiles), shots)
         for s in range(1, shots):
             factor = jnp.where(lane_row_shot == s, factors[s], factor)
         origin = 2 * lax.rem(group * per_owner, per_pack) + 1
         for h in range(2):
-            halo = factor[0:1] * halves[0, h]
-            for g in range(1, groups):
+            halo = zero
+            for g in sources:
                 halo = halo + factor[g:g + 1] * halves[g, h]
             for i in range(owned):
                 for t in range(tiles):
@@ -338,13 +378,24 @@
                     here = pl.ds((h * tiles + t) * SUBLANES, SUBLANES)
                     out_ref[i, here] = out_ref[i, here] - jnp.where(ends, value, 0.0)
 
+    @pl.when(group < early)
+    def _():
+        correct(range(groups))
+
+    for sources, target in pairs:
+        @pl.when(late & (group == target))
+        def _():
+            correct(sources)
+
     pltpu.make_async_copy(inbox.at[pl.ds(0, devices - 1)], inbox.at[pl.ds(0, devices - 1)], note_send).wait()
     for g in range(early):
-        sent = min(g + 1, early)
-
-        @pl.when((group == g + 1) if g + 1 < early else (group > g))
-        def _():
-            pltpu.make_async_copy(halo_in.at[pl.ds(0, sent)], halo_in.at[pl.ds(0, sent)], edge_send).wait()
+        for extra in (False, True):
+            sent = min(g + 1, early) + extra
+
+            @pl.when(((group == g + 1) if g + 1 < early else (group > g)) & (any_ahead == extra))
+            def _():
+                pltpu.make_async_copy(halo_in.at[pl.ds(0, sent)], halo_in.at[pl.ds(0, sent)], edge_send).wait()
+
     others = send.at[pl.ds(0, groups - 1)]
     pltpu.make_async_copy(others, others, bulk_send).wait()
 
@@ -377,6 +428,7 @@
             pltpu.VMEM((packs, SUBLANES, LANES), f32),
             pltpu.VMEM((groups, SUBLANES, LANES), f32),
             pltpu.VMEM((groups, 2, SUBLANES, LANES), f32),
+            pltpu.VMEM(block, f32),
             pltpu.VMEM((groups,) + block, f32),
             pltpu.VMEM((groups,) + block, f32),
             pltpu.VMEM((SUBLANES, LANES), f32),

time: 13.4 us -> 13.1 us (0.978)
  Pallas kernels: 12.6 us -> 12.3 us
    pallas_call x1, Pallas kernels: 12.6 us -> 12.3 us  [on_device(): pl.pallas_call(functools.partial(kernel, dims), out_shape=pltpu.VMEM((own...]
where the time goes in v5:
time: 13.1 us; the launch traced here: 12.9 us
  Pallas kernels  12.3 us (94%)
  local copies, waits for them, and re-layouts  0.62 us (5%)
    pallas_call x1, Pallas kernels, on_device(): pl.pallas_call(functools.partial(kernel, dims), out_shape=pltpu.VMEM((own...  12.3 us
    unnamed x1, local copies, waits for them, and re-layouts  0.62 us

profile of v5, /device:TPU:29, one launch (start us, length us, event | category | flops | bytes accessed | tf_op | source)
XLA Modules:
  0.0 12.9 jit_solution(6100364936451251523)
XLA Ops:
  0.0 12.3 %shard_map.37 = f32[2,32,128]{2,1,0:T(8,128)S(1)} custom-call(f32[2,16,32,128]{3,2,1,0:T(8,128)} %corr_hbm.1, f32[2,16,32,128]{3,2,1,0:T(8,128)} %ill_hbm.1, s32[2,4]{1,0:T(2,128)} %box_hbm.1), custom_call_target="tpu_custom_call" | custom-call | tf_op jit(solution)/shard_map/pallas_call | solution.py:416
  12.3 0.6 %copy.5 = f32[2,32,128]{2,1,0:T(8,128)} copy(f32[2,32,128]{2,1,0:T(8,128)S(1)} %shard_map.37) | data formatting | bytes 65536

commit v6 on v5

--- a/solution.py
+++ b/solution.py
@@ -244,6 +244,10 @@
             src_ref=message.at[pl.ds(0, 1)], dst_ref=inbox.at[pl.ds(slot, 1)], send_sem=note_send, recv_sem=note_recv,
             device_id={"shot": g, "depth": d}, device_id_type=MESH).start()
 
+    @pl.when((group > early) & (depth == 0))
+    def _():
+        bulk(early, group).start()
+
     pl.semaphore_wait(passed, slabs - 1)
     for g in range(groups):
         @pl.when(g < group)
@@ -265,7 +269,7 @@
             halo_copy(target).start()
 
     for g in range(early, groups):
-        @pl.when((g < group) & jnp.logical_not(ahead[1] & (g == pairs[1][1])))
+        @pl.when((g < group) & jnp.logical_not((ahead[1] & (g == pairs[1][1])) | ((depth == 0) & (g == early))))
         def _():
             bulk(g, group).start()
     for g in sorted(range(1, groups), key=lambda g: (g % 2, g) if 2 * g >= groups else (2, g)):
@@ -348,17 +352,20 @@
         peak = jnp.maximum(peak, by_shot[s])
     peak = 0.5 * jnp.max(peak, axis=0, keepdims=True) + 1.0
     factors = [(1.0 / math.sqrt(shots * groups)) / jnp.sqrt(by_shot[s] + peak) for s in range(shots)]
-    for i in range(owned):
-        for t in range(2 * tiles):
-            total_t = None
-            for s in range(shots):
-                part = factors[s][0:1] * spread[0, s, i, pl.ds(t * SUBLANES, SUBLANES)]
-                for g in range(1, groups):
-                    part = part + factors[s][g:g + 1] * spread[g, s, i, pl.ds(t * SUBLANES, SUBLANES)]
-                total_t = part if total_t is None else total_t + part
-            out_ref[i, pl.ds(t * SUBLANES, SUBLANES)] = total_t
+    def weigh(sources):
+        notes = correct(sources) if sources else None
+        for i in range(owned):
+            for t in range(2 * tiles):
+                total_t = None
+                for s in range(shots):
+                    part = factors[s][0:1] * spread[0, s, i, pl.ds(t * SUBLANES, SUBLANES)]
+                    for g in range(1, groups):
+                        part = part + factors[s][g:g + 1] * spread[g, s, i, pl.ds(t * SUBLANES, SUBLANES)]
+                    total_t = part if total_t is None else total_t + part
+                out_ref[i, pl.ds(t * SUBLANES, SUBLANES)] = total_t - notes[i][t] if notes else total_t
 
     def correct(sources):
+        notes = [[zero] * (2 * tiles) for i in range(owned)]
         factor = factors[0]
         lane_row_shot = lax.rem(lax.broadcasted_iota(jnp.int32, (groups, LANES), 1) // (2 * tiles), shots)
         for s in range(1, shots):
@@ -375,17 +382,15 @@
                         shift = 2 * LANES - origin - 2 * ((i * shots + s) * tiles + t)
                         moved = pltpu.roll(halo, shift, 1)
                         value = moved if value is None else value + moved
-                    here = pl.ds((h * tiles + t) * SUBLANES, SUBLANES)
-                    out_ref[i, here] = out_ref[i, here] - jnp.where(ends, value, 0.0)
-
-    @pl.when(group < early)
-    def _():
-        correct(range(groups))
-
-    for sources, target in pairs:
-        @pl.when(late & (group == target))
-        def _():
-            correct(sources)
+                    notes[i][h * tiles + t] = jnp.where(ends, value, 0.0)
+        return notes
+
+    noted = [(group < early, range(groups))] + [(late & (group == target), sources) for sources, target in pairs]
+    plain = jnp.logical_not(noted[0][0] | noted[1][0] | noted[2][0])
+    for here, sources in noted + [(plain, None)]:
+        @pl.when(here)
+        def _():
+            weigh(sources)
 
     pltpu.make_async_copy(inbox.at[pl.ds(0, devices - 1)], inbox.at[pl.ds(0, devices - 1)], note_send).wait()
     for g in range(early):

time: 13.1 us -> 13.1 us (level)
  no operation moved by 1% of the time
where the time goes in v6:
time: 13.1 us; the launch traced here: 12.9 us
  Pallas kernels  12.3 us (94%)
  local copies, waits for them, and re-layouts  0.62 us (5%)
    pallas_call x1, Pallas kernels, on_device(): pl.pallas_call(functools.partial(kernel, dims), out_shape=pltpu.VMEM((own...  12.3 us
    unnamed x1, local copies, waits for them, and re-layouts  0.62 us

profile of v6, /device:TPU:29, one launch (start us, length us, event | category | flops | bytes accessed | tf_op | source)
XLA Modules:
  0.0 12.9 jit_solution(11007230570947711464)
XLA Ops:
  0.0 12.3 %shard_map.37 = f32[2,32,128]{2,1,0:T(8,128)S(1)} custom-call(f32[2,16,32,128]{3,2,1,0:T(8,128)} %corr_hbm.1, f32[2,16,32,128]{3,2,1,0:T(8,128)} %ill_hbm.1, s32[2,4]{1,0:T(2,128)} %box_hbm.1), custom_call_target="tpu_custom_call" | custom-call | tf_op jit(solution)/shard_map/pallas_call | solution.py:421
  12.3 0.6 %copy.5 = f32[2,32,128]{2,1,0:T(8,128)} copy(f32[2,32,128]{2,1,0:T(8,128)S(1)} %shard_map.37) | data formatting | bytes 65536

commit v7 on v6

--- a/solution.py
+++ b/solution.py
@@ -32,7 +32,7 @@
     box_copy.start()
     for s in range(shots):
         for source, target in ((corr_hbm, corr), (ill_hbm, ill)):
-            pltpu.make_async_copy(source.at[s], target.at[s], note_send).start()
+            pltpu.make_async_copy(source.at[s], target.at[s], (note_send, edge_send)[s % 2]).start()
 
     def signal(semaphore, **device):
         pl.semaphore_signal(semaphore, inc=1, device_id=device, device_id_type=MESH)
@@ -72,15 +72,17 @@
         start.append(jnp.minimum(first, half))
         lower.append([(sub + t * SUBLANES >= first) & (sub + t * SUBLANES < last) for t in range(tiles)])
         upper.append([(sub + t * SUBLANES + half >= first) & (sub + t * SUBLANES + half < last) for t in range(tiles)])
-    pltpu.make_async_copy(raw, raw, note_send).wait()
 
     def lane_of(r, s, t):
         k = (r * shots + s) * tiles + t
         return k // per_pack, 2 * (k % per_pack)
 
     packed = [zero] * packs
-    for r in range(rows):
-        for s in range(shots):
+    for s in range(shots):
+        if s < 2:
+            pair = raw.at[:, pl.ds(0, len(range(s, shots, 2)))]
+            pltpu.make_async_copy(pair, pair, (note_send, edge_send)[s]).wait()
+        for r in range(rows):
             in_row = (r >= box[s, 0]) & (r < box[s, 1])
             parts = []
             for t in range(tiles):
@@ -179,19 +181,23 @@
             recv_sem=halo_recv, device_id={"shot": g}, device_id_type=MESH)
 
     early = min(EARLY, groups)
-    for g in range(early):
-        @pl.when(g < group)
-        def _():
-            bulk(g, group).start()
-
     quarter = groups // 4
     pairs = ((range(quarter, 2 * quarter), 2 * quarter), (range(2 * quarter, 3 * quarter), quarter))
     ahead = [late & (group >= sources[0]) & (group <= sources[-1]) for sources, target in pairs]
+    for here, (sources, target) in zip(ahead, pairs):
+        @pl.when(here)
+        def _():
+            spare[...] = send[target]
+
+    for g in range(early):
+        @pl.when(g < group)
+        def _():
+            bulk(g, group).start()
+
     any_ahead = ahead[0] | ahead[1]
     for here, (sources, target) in zip(ahead, pairs):
         @pl.when(here)
         def _():
-            spare[...] = send[target]
             if target > sources[0]:
                 pl.semaphore_wait(ready.at[target - 1], 1)
             pltpu.make_async_remote_copy(

time: 13.1 us -> 13 us (level)
  no operation moved by 1% of the time
where the time goes in v7:
time: 13 us; the launch traced here: 12.9 us
  Pallas kernels  12.3 us (95%)
  local copies, waits for them, and re-layouts  0.62 us (5%)
    pallas_call x1, Pallas kernels, on_device(): pl.pallas_call(functools.partial(kernel, dims), out_shape=pltpu.VMEM((own...  12.3 us
    unnamed x1, local copies, waits for them, and re-layouts  0.62 us

profile of v7, /device:TPU:29, one launch (start us, length us, event | category | flops | bytes accessed | tf_op | source)
XLA Modules:
  0.0 12.9 jit_solution(10704065201921226145)
XLA Ops:
  0.0 12.3 %shard_map.37 = f32[2,32,128]{2,1,0:T(8,128)S(1)} custom-call(f32[2,16,32,128]{3,2,1,0:T(8,128)} %corr_hbm.1, f32[2,16,32,128]{3,2,1,0:T(8,128)} %ill_hbm.1, s32[2,4]{1,0:T(2,128)} %box_hbm.1), custom_call_target="tpu_custom_call" | custom-call | tf_op jit(solution)/shard_map/pallas_call | solution.py:427
  12.3 0.6 %copy.5 = f32[2,32,128]{2,1,0:T(8,128)} copy(f32[2,32,128]{2,1,0:T(8,128)S(1)} %shard_map.37) | data formatting | bytes 65536

commit v8 on v7

--- a/solution.py
+++ b/solution.py
@@ -341,6 +341,18 @@
         def _():
             collect(sources, len(sources))
 
+    pltpu.make_async_copy(inbox.at[pl.ds(0, devices - 1)], inbox.at[pl.ds(0, devices - 1)], note_send).wait()
+    for g in range(early):
+        for extra in (False, True):
+            sent = min(g + 1, early) + extra
+
+            @pl.when(((group == g + 1) if g + 1 < early else (group > g)) & (any_ahead == extra))
+            def _():
+                pltpu.make_async_copy(halo_in.at[pl.ds(0, sent)], halo_in.at[pl.ds(0, sent)], edge_send).wait()
+
+    others = send.at[pl.ds(0, groups - 1)]
+    pltpu.make_async_copy(others, others, bulk_send).wait()
+
     pltpu.make_async_copy(inbox, inbox, note_recv).wait()
     meansq = inbox[pl.ds(0, groups)]
     for d in range(1, slabs):
@@ -397,18 +409,6 @@
         @pl.when(here)
         def _():
             weigh(sources)
-
-    pltpu.make_async_copy(inbox.at[pl.ds(0, devices - 1)], inbox.at[pl.ds(0, devices - 1)], note_send).wait()
-    for g in range(early):
-        for extra in (False, True):
-            sent = min(g + 1, early) + extra
-
-            @pl.when(((group == g + 1) if g + 1 < early else (group > g)) & (any_ahead == extra))
-            def _():
-                pltpu.make_async_copy(halo_in.at[pl.ds(0, sent)], halo_in.at[pl.ds(0, sent)], edge_send).wait()
-
-    others = send.at[pl.ds(0, groups - 1)]
-    pltpu.make_async_copy(others, others, bulk_send).wait()
 
 
 def on_device(correlation, illumination, aperture):

time: 13 us -> 13 us (level)
  no operation moved by 1% of the time
where the time goes in v8:
time: 13 us; the launch traced here: 12.9 us
  Pallas kernels  12.3 us (95%)
  local copies, waits for them, and re-layouts  0.62 us (5%)
    pallas_call x1, Pallas kernels, on_device(): pl.pallas_call(functools.partial(kernel, dims), out_shape=pltpu.VMEM((own...  12.3 us
    unnamed x1, local copies, waits for them, and re-layouts  0.62 us

profile of v8, /device:TPU:29, one launch (start us, length us, event | category | flops | bytes accessed | tf_op | source)
XLA Modules:
  0.0 12.9 jit_solution(17839954138659070342)
XLA Ops:
  0.0 12.3 %shard_map.37 = f32[2,32,128]{2,1,0:T(8,128)S(1)} custom-call(f32[2,16,32,128]{3,2,1,0:T(8,128)} %corr_hbm.1, f32[2,16,32,128]{3,2,1,0:T(8,128)} %ill_hbm.1, s32[2,4]{1,0:T(2,128)} %box_hbm.1), custom_call_target="tpu_custom_call" | custom-call | tf_op jit(solution)/shard_map/pallas_call | solution.py:427
  12.3 0.6 %copy.5 = f32[2,32,128]{2,1,0:T(8,128)} copy(f32[2,32,128]{2,1,0:T(8,128)S(1)} %shard_map.37) | data formatting | bytes 65536
